TPU v7x, 128 devices: a whole 4x4x4 slice. The times are simulated.
128 devices in a mesh: det: 4 (over x), tm: 32 (over z, y, core).
Axes of the slice: x: 4, y: 4, z: 4, core: 2. Of those that a mesh axis runs over, the one named last changes fastest.
Arguments:
- sol_map: float32 [3, 196608], P(None, ('det', 'tm')), may hold values from -6 to 6
- resid_map: float32 [3, 196608], P(None, ('det', 'tm')), may hold values from -6 to 6
- direction: float32 [3, 196608], P(None, ('det', 'tm')), may hold values from -6 to 6
- precond: float32 [3, 196608], P(None, ('det', 'tm')), may hold values from 0.1 to 1
- pixels: int32 [128, 65536], P('det', 'tm'), may hold values from 0 to 196607
- angle_index: int32 [128, 65536], P('det', 'tm'), may hold values from 0 to 127
- angles: float32 [128], replicated, may hold values from -3.140625 to 3.140625
- flag_mask: int32 [128, 65536], P('det', 'tm'), may hold values 0 or 1
- inv_noise: float32 [128, 32769], P(('det', 'tm')), may hold values from 0.05 to 1
Outputs:
- new_sol: float32 [3, 196608], P(None, ('det', 'tm'))
- new_resid: float32 [3, 196608], P(None, ('det', 'tm'))
- new_dir: float32 [3, 196608], P(None, ('det', 'tm'))
- new_norm: float32 [], replicated
All inputs are finite; a program needn't handle non-finite values. No bound on the sum of `flag_mask` on one device may be relied on, other than what follows from the above.
Results may differ from a plain program's by a relative error of at most 0.0001.
Values sent between devices are 32-bit elements; how exact they have to be, the bound alone decides.
No kernel may reach another device: no remote copies, remote signals or barrier semaphores. Data moves between devices by JAX's collectives and lax.ppermute only.
A program may use at most 320 MiB of HBM per device.

v0:
```python
import functools
import math

import jax
import jax.numpy as jnp
import numpy as np
from jax import lax
from jax.experimental import pallas as pl
from jax.experimental.pallas import tpu as pltpu
from jax.sharding import Mesh
from jax.sharding import PartitionSpec as P

DET_TM = ("det", "tm_0", "tm_1", "tm_2")
TM = ("tm_0", "tm_1", "tm_2")
CHIPS = ("det", "tm_0", "tm_1")
CORE = "tm_2"

LANES = 128
CHUNK = 256
WINDOW = 16
ROWS = 16
VMEM = pl.BlockSpec(memory_space=pltpu.VMEM)
SMEM = pl.BlockSpec(memory_space=pltpu.SMEM)


def exchange(array, axes):
    return lax.all_to_all(array, axes, split_axis=0, concat_axis=0, tiled=True)


def halves(values):
    high = values.astype(jnp.bfloat16)
    return high, (values - high.astype(jnp.float32)).astype(jnp.bfloat16)


def dot(left, right, dims=(((1,), (0,)), ((), ()))):
    return lax.dot_general(left, right, dims, preferred_element_type=jnp.float32)


def dot3(left, right):
    return dot(left[0], right[0]) + (dot(left[0], right[1]) + dot(left[1], right[0]))


LEVELS = 16
CHUNK_BITS = 8
TILES = 64
SLOTS = LEVELS * (LEVELS - 1) + 2 * LEVELS


def tile(ref, index):
    return ref.at[8 * index : 8 * index + 8, :]


def partner(values, bit):
    axis, size, step = (0, 8, 1 << (bit - 5)) if bit < 8 else (1, LANES, 1 << (bit - 9))
    if 2 * step == size:
        return pltpu.roll(values, step, axis)
    upper = (lax.broadcasted_iota(jnp.int32, (8, LANES), axis) & step) != 0
    return jnp.where(upper, pltpu.roll(values, step, axis), pltpu.roll(values, size - step, axis))


def tile_pairs(bit):
    step = 1 << (5 if bit == 8 else bit)
    return [(i, i + step) for i in range(TILES) if not i & step]


def is_tile_bit(bit):
    return bit < 5 or bit == 8


def word(position):
    return jnp.int32(-(1 << 31) if position == 31 else 1 << position)


def slot(level, bit):
    return level * (level - 1) + 2 * bit


def in_network(level, bit):
    return jnp.logical_and(bit < level, jnp.logical_or(level < LEVELS, bit >= CHUNK_BITS))


def place(tile_index):
    inside = lax.broadcasted_iota(jnp.int32, (8, LANES), 0) * 32 + lax.broadcasted_iota(jnp.int32, (8, LANES), 1) * 512
    return inside + ((tile_index & 31) + ((tile_index >> 5) << 8))


def sort_stage(key_ref, mask_ref, level, bit):
    at = slot(level, bit)
    if is_tile_bit(bit):
        bits = jnp.zeros((8, LANES), jnp.int32)
        for position, (low, high) in enumerate(tile_pairs(bit)):
            a, b = tile(key_ref, low)[...], tile(key_ref, high)[...]
            swap = a > b
            tile(key_ref, low)[...] = jnp.where(swap, b, a)
            tile(key_ref, high)[...] = jnp.where(swap, a, b)
            bits = bits | jnp.where(swap, word(position), 0)
        mask_ref[at] = bits
        return
    axis, step = (0, 1 << (bit - 5)) if bit < 8 else (1, 1 << (bit - 9))
    upper = -((lax.broadcasted_iota(jnp.int32, (8, LANES), axis) & step) // step)
    for part in range(2):
        bits = jnp.zeros((8, LANES), jnp.int32)
        for position in range(32):
            view = tile(key_ref, 32 * part + position)
            own = view[...]
            other = partner(own, bit)
            swap = (own ^ upper) > (other ^ upper)
            view[...] = jnp.where(swap, other, own)
            bits = bits | jnp.where(swap, word(position), 0)
        mask_ref[at + part] = bits


def replay_stage(data_ref, mask_ref, level, bit):
    at = slot(level, bit)
    if is_tile_bit(bit):
        bits = mask_ref[at]
        for position, (low, high) in enumerate(tile_pairs(bit)):
            a, b = tile(data_ref, low)[...], tile(data_ref, high)[...]
            swap = (bits & word(position)) != 0
            tile(data_ref, low)[...] = jnp.where(swap, b, a)
            tile(data_ref, high)[...] = jnp.where(swap, a, b)
        return
    for part in range(2):
        bits = mask_ref[at + part]
        for position in range(32):
            view = tile(data_ref, 32 * part + position)
            own = view[...]
            view[...] = jnp.where((bits & word(position)) != 0, partner(own, bit), own)


def network(stage, backwards=False, before=None):
    def one_level(count, carry):
        level = LEVELS - count if backwards else count + 1
        if before is not None:
            before(level)
        for bit in range(LEVELS) if backwards else reversed(range(LEVELS)):
            pl.when(in_network(level, bit))(functools.partial(stage, level, bit))
        return carry

    lax.fori_loop(0, LEVELS, one_level, 0)


def sort_kernel(pointing_ref, trig_ref, pix_ref, weight_ref, bound_ref, mask_ref, key_ref):
    blocks, _, block_rows, _ = pointing_ref.shape
    for block in range(blocks):
        packed = pointing_ref[block, 0] * 256 + pointing_ref[block, 1] * 2 + pointing_ref[block, 2]
        key_ref[block * block_rows : (block + 1) * block_rows, :] = packed
    for index in range(TILES):
        tile(key_ref, index)[...] ^= -(place(index) & 1)

    def turn(level):
        for index in range(TILES):
            at = place(index)
            tile(key_ref, index)[...] ^= -(((at >> level) ^ (at >> (level - 1))) & 1)

    network(functools.partial(sort_stage, key_ref, mask_ref), before=turn)

    half = key_ref.shape[0] // 2
    for h in range(2):
        keys = key_ref[h * half : (h + 1) * half, :]
        bound_ref[h : h + 1, :] = jnp.min(keys, axis=0, keepdims=True) >> 8
        bound_ref[2 + h : 3 + h, :] = jnp.max(keys, axis=0, keepdims=True) >> 8
    cos_row = jnp.broadcast_to(trig_ref[0:1, :], (8, LANES))
    sin_row = jnp.broadcast_to(trig_ref[1:2, :], (8, LANES))
    for part in range(4):
        keys = key_ref[part * LANES : (part + 1) * LANES, :].T
        cols = slice(part * LANES, (part + 1) * LANES)
        pix_ref[:, cols] = keys >> 8
        for row in range(0, LANES, 8):
            key = keys[row : row + 8]
            angle = (key >> 1) & (LANES - 1)
            usable = (key & 1).astype(jnp.float32)
            weight_ref[0, row : row + 8, cols] = usable
            weight_ref[1, row : row + 8, cols] = usable * jnp.take_along_axis(cos_row, angle, axis=1, mode="promise_in_bounds")
            weight_ref[2, row : row + 8, cols] = usable * jnp.take_along_axis(sin_row, angle, axis=1, mode="promise_in_bounds")


def one_hot_low(pixel_row):
    low = (pixel_row & (LANES - 1)).astype(jnp.float32).astype(jnp.bfloat16)
    level = lax.broadcasted_iota(jnp.int32, (LANES, CHUNK), 0).astype(jnp.float32).astype(jnp.bfloat16)
    return jnp.where(jnp.broadcast_to(low, level.shape) == level, jnp.bfloat16(1.0), jnp.bfloat16(0.0))


def window_mask(pixel_row, base):
    level = lax.broadcasted_iota(jnp.int32, (WINDOW, CHUNK), 0)
    return ((pixel_row >> 7) - base) == level


def gather_window(tab_ref, pixel_row, weight_rows, base):
    pieces = []
    for comp in range(3):
        pieces.extend(halves(tab_ref[comp, pl.ds(base, WINDOW), :]))
    found = dot(jnp.concatenate(pieces, axis=0), one_hot_low(pixel_row))
    total = None
    for comp in range(3):
        lo = 2 * comp * WINDOW
        value = (found[lo : lo + WINDOW] + found[lo + WINDOW : lo + 2 * WINDOW]) * weight_rows[comp]
        total = value if total is None else total + value
    return jnp.sum(jnp.where(window_mask(pixel_row, base), total, 0.0), axis=0, keepdims=True)


def first_base(bound_ref, row, half):
    return pl.multiple_of((bound_ref[half, row] >> 10) << 3, 8)


def window_count(bound_ref, row, half):
    return (((bound_ref[2 + half, row] >> 7) - first_base(bound_ref, row, half)) >> 4) + 1


def more_windows(bound_ref, head, one):
    counts = [window_count(bound_ref, head + r, h) for r in range(ROWS) for h in range(2)]

    @pl.when(functools.reduce(jnp.maximum, counts) > 1)
    def _():
        def each(r, carry):
            for h in range(2):
                base = first_base(bound_ref, head + r, h)

                def more(w, inner, h=h, base=base):
                    one(head + r, h, pl.multiple_of(base + w * WINDOW, 8))
                    return inner

                lax.fori_loop(1, window_count(bound_ref, head + r, h), more, 0)
            return carry

        lax.fori_loop(0, ROWS, each, 0)


def cut(values, r, h):
    return values[r : r + 1, h * CHUNK : (h + 1) * CHUNK]


def held(ref, row, h, *lead):
    return ref[(*lead, pl.ds(row, 1), slice(h * CHUNK, (h + 1) * CHUNK))]


def gather_all(bound_ref, pix_ref, weight_ref, tab_ref, out_ref):
    def step(it, carry):
        head = pl.multiple_of(it * ROWS, 8)
        pix = pix_ref[pl.ds(head, ROWS), :]
        weights = [weight_ref[comp, pl.ds(head, ROWS), :] for comp in range(3)]
        rows = []
        for r in range(ROWS):
            parts = [
                gather_window(tab_ref, cut(pix, r, h), [cut(w, r, h) for w in weights], first_base(bound_ref, head + r, h)) for h in range(2)
            ]
            rows.append(jnp.concatenate(parts, axis=1))
        out_ref[pl.ds(head, ROWS), :] = jnp.concatenate(rows, axis=0)

        def one(row, h, base):
            value = gather_window(tab_ref, held(pix_ref, row, h), [held(weight_ref, row, h, comp) for comp in range(3)], base)
            out_ref[pl.ds(row, 1), h * CHUNK : (h + 1) * CHUNK] += value

        more_windows(bound_ref, head, one)
        return carry

    lax.fori_loop(0, pix_ref.shape[0] // ROWS, step, 0)


def scatter_window(pixel_row, value_rows, base):
    mask = window_mask(pixel_row, base)
    pieces = []
    for value in value_rows:
        high = value.astype(jnp.bfloat16).astype(jnp.float32)
        for part in (high, value - high):
            pieces.append(jnp.where(mask, part, 0.0).astype(jnp.bfloat16))
    sums = dot(jnp.concatenate(pieces, axis=0), one_hot_low(pixel_row), (((1,), (1,)), ((), ())))
    return [sums[2 * c * WINDOW : (2 * c + 1) * WINDOW] + sums[(2 * c + 1) * WINDOW : (2 * c + 2) * WINDOW] for c in range(3)]


def scatter_all(bound_ref, pix_ref, weight_ref, value_ref, map_ref):
    map_ref[...] = jnp.zeros(map_ref.shape, jnp.float32)

    def add(sums, base):
        for comp in range(3):
            map_ref[comp, pl.ds(base, WINDOW), :] += sums[comp]

    def step(it, carry):
        head = pl.multiple_of(it * ROWS, 8)
        pix = pix_ref[pl.ds(head, ROWS), :]
        value = value_ref[pl.ds(head, ROWS), :]
        contrib = [value * weight_ref[comp, pl.ds(head, ROWS), :] for comp in range(3)]
        places = [(r, h) for r in range(ROWS) for h in range(2)]
        bases = [first_base(bound_ref, head + r, h) for r, h in places]
        sums = [scatter_window(cut(pix, r, h), [cut(c, r, h) for c in contrib], base) for (r, h), base in zip(places, bases)]
        for base, one_sum in zip(bases, sums):
            add(one_sum, base)

        def one(row, h, base):
            value = held(value_ref, row, h)
            add(scatter_window(held(pix_ref, row, h), [value * held(weight_ref, row, h, c) for c in range(3)], base), base)

        more_windows(bound_ref, head, one)
        return carry

    lax.fori_loop(0, pix_ref.shape[0] // ROWS, step, 0)


def main_kernel(
    bound_ref, tail_ref, pix_ref, weight_ref, mask_ref, full_ref, form_ref, twist_ref, filt_ref, out_ref, tab_ref, series_ref, wide_ref
):
    share_rows = full_ref.shape[1] // 3
    map_rows = full_ref.shape[0] * share_rows

    def lay(couple, carry):
        row = pl.multiple_of(couple * 2 * share_rows, 8)
        for comp in range(3):
            parts = [full_ref[2 * couple + h, comp * share_rows : (comp + 1) * share_rows, :] for h in range(2)]
            tab_ref[comp, pl.ds(row, 2 * share_rows), :] = jnp.concatenate(parts, axis=0)
        return carry

    lax.fori_loop(0, full_ref.shape[0] // 2, lay, 0)
    tab_ref[:, map_rows:, :] = jnp.zeros((3, tab_ref.shape[1] - map_rows, LANES), jnp.float32)

    gather_all(bound_ref, pix_ref, weight_ref, tab_ref, wide_ref)
    for part in range(4):
        series_ref[part * LANES : (part + 1) * LANES, :] = wide_ref[:, part * LANES : (part + 1) * LANES].T
    network(functools.partial(replay_stage, series_ref, mask_ref), backwards=True)
    filter_series(form_ref, twist_ref, filt_ref, tail_ref, series_ref)
    network(functools.partial(replay_stage, series_ref, mask_ref))
    for part in range(4):
        wide_ref[:, part * LANES : (part + 1) * LANES] = series_ref[part * LANES : (part + 1) * LANES, :].T
    scatter_all(bound_ref, pix_ref, weight_ref, wide_ref, tab_ref)

    def spread(chip, carry):
        row = pl.multiple_of(chip * 2 * share_rows, 8)
        for comp in range(3):
            both = tab_ref[comp, pl.ds(row, 2 * share_rows), :]
            for core in range(2):
                out_ref[core, chip, comp * share_rows : (comp + 1) * share_rows, :] = both[core * share_rows : (core + 1) * share_rows]
        return carry

    lax.fori_loop(0, out_ref.shape[1], spread, 0)


def filter_tables(side):
    index = np.arange(side)
    turn = 2.0 * np.pi / side * ((index[:, None] * index[None, :]) % side)
    twist = 2.0 * np.pi / (side * side) * (index[:, None] * index[None, :])

    def split(values):
        high = values.astype(np.float32).astype(jnp.bfloat16)
        return high, (values - high.astype(np.float64)).astype(np.float32).astype(jnp.bfloat16)

    forms = np.stack([*split(np.cos(turn)), *split(-np.sin(turn))])
    twists = np.stack([np.cos(twist), -np.sin(twist)]).astype(np.float32)
    return forms, twists


def filter_series(form_ref, twist_ref, weight_ref, tail_ref, x_ref):
    side = form_ref.shape[1]
    half = side // 2
    total = side * side
    f_real = (form_ref[0], form_ref[1])
    f_imag = (form_ref[2], form_ref[3])
    w_real, w_imag = twist_ref[0], twist_ref[1]
    x = jnp.concatenate([x_ref[pl.ds(0, side, 2), :], x_ref[pl.ds(1, side, 2), :]], axis=1)
    xs = halves(x)
    y_real = dot3(f_real, xs)
    y_imag = dot3(f_imag, xs)
    y_real, y_imag = halves(y_real * w_real - y_imag * w_imag), halves(y_real * w_imag + y_imag * w_real)
    left_real = (f_real[0][:, :half], f_real[1][:, :half])
    left_imag = (f_imag[0][:, :half], f_imag[1][:, :half])
    weight = weight_ref[...]
    z_real = halves((dot3(y_real, left_real) - dot3(y_imag, left_imag)) * weight)
    z_imag = halves((dot3(y_real, left_imag) + dot3(y_imag, left_real)) * weight)
    top_real = (f_real[0][:half], f_real[1][:half])
    top_imag = (f_imag[0][:half], f_imag[1][:half])
    v_real = dot3(z_real, top_real) + dot3(z_imag, top_imag)
    v_imag = dot3(z_imag, top_real) - dot3(z_real, top_imag)
    v_real, v_imag = halves(v_real * w_real + v_imag * w_imag), halves(v_imag * w_real - v_real * w_imag)
    result = dot3(f_real, v_real) + dot3(f_imag, v_imag)
    sign = jnp.where((lax.broadcasted_iota(jnp.int32, (1, side), 1) & 1) == 0, 1.0, -1.0)
    last = jnp.sum(jnp.sum(x, axis=0, keepdims=True) * sign, axis=1, keepdims=True) * tail_ref[0]
    result = (result + last * sign) * (1.0 / total)
    x_ref[pl.ds(0, side, 2), :] = result[:, :half]
    x_ref[pl.ds(1, side, 2), :] = result[:, half:]


def body(sol_map, resid_map, direction, precond, pixels, angle_index, angles, flag_mask, inv_noise, forms, twists):
    share_len = direction.shape[1]
    n_dev = lax.axis_size(DET_TM)
    n_pixels = share_len * n_dev
    map_rows = n_pixels // LANES
    share_rows = share_len // LANES
    det_rows, samples = pixels.shape
    total = det_rows * samples
    side = math.isqrt(total)
    f32 = jnp.float32

    pointing = jnp.stack([a.reshape(det_rows, samples // LANES, LANES) for a in (pixels, angle_index, flag_mask)], axis=1)
    pointing = exchange(pointing, TM)

    own = direction.reshape(1, 3 * share_rows, LANES)
    full = exchange(jnp.broadcast_to(own, (n_dev, 3 * share_rows, LANES)), DET_TM)

    trig = jnp.stack([jnp.cos(2.0 * angles), jnp.sin(2.0 * angles)])
    wide = (LANES, total // LANES)
    pix, weights, bounds, masks = pl.pallas_call(
        sort_kernel,
        in_specs=[VMEM, VMEM],
        out_specs=[VMEM] * 4,
        out_shape=[
            jax.ShapeDtypeStruct(wide, jnp.int32),
            jax.ShapeDtypeStruct((3, *wide), f32),
            jax.ShapeDtypeStruct((4, LANES), jnp.int32),
            jax.ShapeDtypeStruct((SLOTS, 8, LANES), jnp.int32),
        ],
        scratch_shapes=[pltpu.VMEM((total // LANES, LANES), jnp.int32)],
    )(pointing, trig)

    doubled = inv_noise[0, : total // 2].reshape(side // 2, side).T * 2.0
    corner = jnp.zeros((side, side // 2), jnp.bool_).at[0, 0].set(True)
    doubled = jnp.where(corner, inv_noise[0, 0], doubled)
    shares = pl.pallas_call(
        main_kernel,
        in_specs=[SMEM, SMEM] + [VMEM] * 7,
        out_specs=VMEM,
        out_shape=jax.ShapeDtypeStruct((2, n_dev // 2, 3 * share_rows, LANES), f32),
        scratch_shapes=[pltpu.VMEM((3, map_rows + 8, LANES), f32), pltpu.VMEM((total // LANES, LANES), f32), pltpu.VMEM(wide, f32)],
    )(bounds, inv_noise[0, total // 2 :], pix, weights, masks, full, forms, twists, doubled)

    shares = jnp.sum(exchange(shares, CORE), axis=0)
    image = jnp.sum(exchange(shares, CHIPS), axis=0).reshape(3, share_len)

    scaled_resid = precond * resid_map
    scalars = jnp.stack(
        [
            jnp.sum(scaled_resid * resid_map),
            jnp.sum(direction * image),
            jnp.sum(image * scaled_resid),
            jnp.sum(image * precond * image),
        ]
    )
    scalars = jnp.pad(scalars, (0, LANES - 4)).reshape(1, 1, LANES)
    scalars = jnp.sum(exchange(jnp.broadcast_to(scalars, (n_dev, 1, LANES)), DET_TM), axis=(0, 1))
    norm_old, curvature, cross_term, image_norm = scalars[0], scalars[1], scalars[2], scalars[3]
    step_size = norm_old / curvature
    new_resid = resid_map - step_size * image
    new_norm = norm_old - 2.0 * step_size * cross_term + step_size * step_size * image_norm
    new_sol = sol_map + step_size * direction
    new_dir = precond * new_resid + new_norm / norm_old * direction
    return (new_sol, new_resid, new_dir, new_norm)


def solution(mesh):
    split = Mesh(mesh.devices.reshape(mesh.shape["det"], 4, 4, 2), DET_TM)
    mapped = jax.shard_map(
        body,
        mesh=split,
        in_specs=(
            P(None, DET_TM),
            P(None, DET_TM),
            P(None, DET_TM),
            P(None, DET_TM),
            P("det", TM),
            P("det", TM),
            P(),
            P("det", TM),
            P(DET_TM, None),
            P(),
            P(),
        ),
        out_specs=(P(None, DET_TM), P(None, DET_TM), P(None, DET_TM), P()),
        check_vma=False,
    )

    def run(sol_map, resid_map, direction, precond, pixels, angle_index, angles, flag_mask, inv_noise):
        forms, twists = filter_tables(math.isqrt(pixels.shape[1]))
        return mapped(
            sol_map, resid_map, direction, precond, pixels, angle_index, angles, flag_mask, inv_noise, jnp.asarray(forms), jnp.asarray(twists)
        )

    return run
```

profile of v0, /device:TPU:1, one launch (start us, length us, event | category | flops | bytes accessed | tf_op | source)
XLA Modules:
  0.0 171.9 jit_solution(6192797246396512868)
XLA Ops:
  0.6 0.0 copy-start.2
  0.6 1.0 copy.32
  1.6 1.0 copy.31
  2.7 1.0 copy.30
  3.7 0.9 pad_add_fusion
  4.6 9.6 %all-to-all-start = ((s32[32,3,16,128]{3,2,1,0:T(8,128)}), s32[32,3,16,128]{3,2,1,0:T(8,128)S(1)}, u32[]{:S(2)}, u32[]{:S(2)}) async-start(s32[32,3,16,128]{3,2,1,0:T(8,128)} %pad_add_fusion), calls=%async_computation | async-start | bytes 1572864 | tf_op jit(solution)/shard_map/all_to_all | solution.py:27
  14.2 0.0 copy-done.2
  14.2 14.2 %all-to-all-done.pointing_ref = s32[32,3,16,128]{3,2,1,0:T(8,128)S(1)} async-done(((s32[32,3,16,128]{3,2,1,0:T(8,128)}), s32[32,3,16,128]{3,2,1,0:T(8,128)S(1)}, u32[]{:S(2)}, u32[]{:S(2)}) %all-to-all-start) | async-done | bytes 786464 | tf_op jit(solution)/shard_map/all_to_all | solution.py:27
  28.4 0.0 copy-start.1
  28.4 1.7 %broadcast_in_dim.18 = f32[128,36,128]{2,1,0:T(8,128)} broadcast(f32[36,128]{1,0:T(8,128)S(1)} %broadcast_in_dim.17), dimensions={1,2} | broadcast | bytes 2377728 | tf_op jit(solution)/shard_map/broadcast_in_dim | solution.py:395
  30.2 0.0 copy-start.4
  30.2 0.0 copy-start.8
  30.2 0.0 copy-done.1
  30.2 5.7 %all-to-all-start.1 = ((f32[128,36,128]{2,1,0:T(8,128)}), f32[128,36,128]{2,1,0:T(8,128)S(1)}, u32[]{:S(2)}, u32[]{:S(2)}) async-start(f32[128,36,128]{2,1,0:T(8,128)} %broadcast_in_dim.18), calls=%async_computation.1 | async-start | bytes 5242880 | tf_op jit(solution)/shard_map/all_to_all | solution.py:27
  35.9 0.0 copy-done.4
  35.9 0.5 fusion.1
  36.4 2.0 %select_reduce_fusion = f32[32768]{0:T(1024)S(1)} fusion(pred[1,32768]{1,0:T(4,128)(4,1)} %constant.46.clone.1, f32[1,32769]{1,0:T(1,128)S(1)} %copy-done.4, f32[]{:T(128)} %bitcast.4), kind=kLoop, calls=%fused_computation.1 | loop fusion | flops 65536 | bytes 294916 | tf_op jit(solution)/shard_map/jit(_where)/select_n | solution.py:414
  38.5 0.7 copy.26
  39.2 0.0 copy-done.8
  39.3 0.6 pad_maximum_fusion.trig_ref
  39.8 14.8 %shard_map.138 = (s32[128,512]{1,0:T(8,128)}, f32[3,128,512]{2,1,0:T(8,128)}, s32[4,128]{1,0:T(4,128)}, s32[272,8,128]{2,1,0:T(8,128)}) custom-call(s32[32,3,16,128]{3,2,1,0:T(8,128)} %copy-done.1, f32[2,128]{1,0:T(2,128)} %pad_maximum_fusion.trig_ref), custom_call_target="tpu_custom_call" | custom-call | tf_op jit(solution)/shard_map/pallas_call | solution.py:399
  54.6 17.2 %all-to-all-done.1.full_ref = f32[128,36,128]{2,1,0:T(8,128)S(1)} async-done(((f32[128,36,128]{2,1,0:T(8,128)}), f32[128,36,128]{2,1,0:T(8,128)S(1)}, u32[]{:S(2)}, u32[]{:S(2)}) %all-to-all-start.1) | async-done | bytes 2359328 | tf_op jit(solution)/shard_map/all_to_all | solution.py:27
  71.8 0.0 copy-start
  71.8 1.5 copy-done
  73.3 39.5 %shard_map.139 = f32[2,64,36,128]{3,2,1,0:T(8,128)} custom-call(s32[4,128]{1,0:T(4,128)} %get-tuple-element.20.bound_ref, f32[1]{0:T(128)} %bitcast.3.tail_ref, s32[128,512]{1,0:T(8,128)} %get-tuple-element.21.pix_ref, f32[3,128,512]{2,1,0:T(8,128)} %get-tuple-element.22.weight_ref, s32[272,8,128]{2,1,0:T(8,128)} %get-tuple-element.23.mask_ref, ...), custom_call_target="tpu_custom_call" | custom-call | tf_op jit(solution)/shard_map/pallas_call | solution.py:415
  112.8 2.2 %copy.27 = f32[2,64,36,128]{3,1,2,0:T(8,128)S(1)} copy(f32[2,64,36,128]{3,2,1,0:T(8,128)} %shard_map.139) | data formatting | bytes 4718592 | tf_op jit(solution)/shard_map/pallas_call | solution.py:415
  115.0 6.5 %all_to_all.25 = f32[2,64,36,128]{3,1,2,0:T(8,128)S(1)} all-to-all(f32[2,64,36,128]{3,1,2,0:T(8,128)S(1)} %copy.27), channel_id=1, replica_groups=mesh['det'=4,'tm_0'=4,'tm_1'=4,'tm_2'=2] {'tm_2'}, dimensions={0} | all-to-all | bytes 4718592 | tf_op jit(solution)/shard_map/all_to_all | solution.py:27
  121.5 0.3 reduce_sum.64
  121.8 0.7 copy.28
  122.5 0.0 copy-start.3
  122.5 0.0 copy-start.5
  122.5 0.0 copy-start.6
  122.6 0.0 copy-start.7
  122.6 24.2 %all_to_all.26 = f32[64,36,128]{2,1,0:T(8,128)S(1)} all-to-all(f32[64,36,128]{2,1,0:T(8,128)S(1)} %copy.28), channel_id=1, replica_groups=mesh['det'=4,'tm_0'=4,'tm_1'=4,'tm_2'=2] {'det','tm_0','tm_1'}, dimensions={0} | all-to-all | bytes 2359296 | tf_op jit(solution)/shard_map/all_to_all | solution.py:27
  146.8 0.1 reduce_sum.65
  146.9 0.0 copy-done.3
  146.9 0.0 copy-done.5
  146.9 0.0 copy-done.6
  146.9 0.6 multiply_reduce_fusion.2
  147.6 2.7 %select_maximum_fusion = f32[128]{0:T(128)S(1)} fusion(f32[1]{0:T(128)} %bitcast.8, f32[1]{0:T(128)} %bitcast.7, f32[1]{0:T(128)} %bitcast.6, f32[1]{0:T(128)} %bitcast), kind=kLoop, calls=%fused_computation.11 | loop fusion | flops 1024 | bytes 528 | tf_op jit(solution)/shard_map/stack | solution.py:427
  150.3 15.2 %all_to_all.27 = f32[128,1,128]{2,1,0:T(1,128)S(1)} all-to-all(f32[128,1,128]{2,1,0:T(1,128)S(1)} %broadcast_in_dim.20), channel_id=1, replica_groups=mesh['det'=4,'tm_0'=4,'tm_1'=4,'tm_2'=2] {'det','tm_0','tm_1','tm_2'}, dimensions={0} | all-to-all | bytes 131072 | tf_op jit(solution)/shard_map/all_to_all | solution.py:27
  165.5 0.6 fusion.2
  170.1 0.0 copy-done.7
  170.1 0.6 multiply_add_fusion
  (6 shorter events, 0.2 us)
Async XLA Ops:
  0.6 13.6 %copy-start.2 = (f32[3,1536]{1,0:T(4,128)S(1)}, f32[3,1536]{1,0:T(4,128)}, u32[]{:S(2)}) copy-start(f32[3,1536]{1,0:T(4,128)} %param.15) | copy-start | bytes 55300
  4.6 23.8 %all-to-all-start = ((s32[32,3,16,128]{3,2,1,0:T(8,128)}), s32[32,3,16,128]{3,2,1,0:T(8,128)S(1)}, u32[]{:S(2)}, u32[]{:S(2)}) async-start(s32[32,3,16,128]{3,2,1,0:T(8,128)} %pad_add_fusion), calls=%async_computation | async-start | bytes 1572864 | tf_op jit(solution)/shard_map/all_to_all | solution.py:27
  28.4 1.7 %copy-start.1 = (s32[32,3,16,128]{3,2,1,0:T(8,128)}, s32[32,3,16,128]{3,2,1,0:T(8,128)S(1)}, u32[]{:S(2)}) copy-start(s32[32,3,16,128]{3,2,1,0:T(8,128)S(1)} %all-to-all-done.pointing_ref) | copy-start | bytes 2359300
  30.2 5.7 %copy-start.4 = (f32[1,32769]{1,0:T(1,128)S(1)}, f32[1,32769]{1,0:T(1,128)}, u32[]{:S(2)}) copy-start(f32[1,32769]{1,0:T(1,128)} %param.21) | copy-start | bytes 393232
  30.2 9.1 %copy-start.8 = (f32[128]{0:T(128)S(1)}, f32[128]{0:T(128)}, u32[]{:S(2)}) copy-start(f32[128]{0:T(128)} %param.19) | copy-start | bytes 1540
  30.2 41.6 %all-to-all-start.1 = ((f32[128,36,128]{2,1,0:T(8,128)}), f32[128,36,128]{2,1,0:T(8,128)S(1)}, u32[]{:S(2)}, u32[]{:S(2)}) async-start(f32[128,36,128]{2,1,0:T(8,128)} %broadcast_in_dim.18), calls=%async_computation.1 | async-start | bytes 5242880 | tf_op jit(solution)/shard_map/all_to_all | solution.py:27
  71.8 1.5 copy-start
  122.5 24.4 %copy-start.3 = (f32[3,1536]{1,0:T(4,128)S(1)}, f32[3,1536]{1,0:T(4,128)}, u32[]{:S(2)}) copy-start(f32[3,1536]{1,0:T(4,128)} %param.15) | copy-start | bytes 55300
  122.5 24.4 %copy-start.5 = (f32[3,1536]{1,0:T(4,128)S(1)}, f32[3,1536]{1,0:T(4,128)}, u32[]{:S(2)}) copy-start(f32[3,1536]{1,0:T(4,128)} %param.16) | copy-start | bytes 55300
  122.5 24.4 %copy-start.6 = (f32[3,1536]{1,0:T(4,128)S(1)}, f32[3,1536]{1,0:T(4,128)}, u32[]{:S(2)}) copy-start(f32[3,1536]{1,0:T(4,128)} %param.14) | copy-start | bytes 55300
  122.6 47.5 %copy-start.7 = (f32[3,1536]{1,0:T(4,128)S(1)}, f32[3,1536]{1,0:T(4,128)}, u32[]{:S(2)}) copy-start(f32[3,1536]{1,0:T(4,128)} %param.13) | copy-start | bytes 55300
where the time goes:
time: 173 us; the launch traced here: 172 us
  Pallas kernels  54.2 us (31%)
  blocking collectives  46 us (27%)
  waiting for transfers between devices  31.4 us (18%)
  starting transfers between devices  15.3 us (9%)
  local copies, waits for them, and re-layouts  11.1 us (6%)
  other arithmetic  7.91 us (5%)
  between operations  5.89 us (3%)
    all_to_all x3, blocking collectives, exchange(): return lax.all_to_all(array, axes, split_axis=0, concat_axis=0, tiled=True)  46 us
    pallas_call x1, Pallas kernels, body(): pl.pallas_call(main_kernel, in_specs=[SMEM, SMEM] + [VMEM] * 7, out_specs...  39.5 us
    all_to_all x2, waiting for transfers between devices, exchange(): return lax.all_to_all(array, axes, split_axis=0, concat_axis=0, tiled=True)  31.4 us
    all_to_all x2, starting transfers between devices, exchange(): return lax.all_to_all(array, axes, split_axis=0, concat_axis=0, tiled=True)  15.3 us
    pallas_call x1, Pallas kernels, body(): pl.pallas_call(sort_kernel, in_specs=[VMEM, VMEM], out_specs=[VMEM] * 4,...  14.8 us
    unnamed x21, local copies, waits for them, and re-layouts  4.55 us
  transfers between devices with their start and end apart: 2, of which 2 were waited for; matrix products, arithmetic and copies ran while one was open for 2% of the time, Pallas kernels for 9%

commit v1 on v0

--- a/solution.py
+++ b/solution.py
@@ -13,6 +13,8 @@
 DET_TM = ("det", "tm_0", "tm_1", "tm_2")
 TM = ("tm_0", "tm_1", "tm_2")
 CHIPS = ("det", "tm_0", "tm_1")
+ROW = "det"
+PLANE = ("tm_0", "tm_1")
 CORE = "tm_2"
 
 LANES = 128
@@ -50,21 +52,34 @@
     return ref.at[8 * index : 8 * index + 8, :]
 
 
+def sublane_step(bit):
+    return 1 << (bit - 5 if bit < 8 else bit - 13)
+
+
+def upper_half(bit):
+    return lax.broadcasted_iota(jnp.int32, (8, LANES), 0) & sublane_step(bit)
+
+
 def partner(values, bit):
-    axis, size, step = (0, 8, 1 << (bit - 5)) if bit < 8 else (1, LANES, 1 << (bit - 9))
-    if 2 * step == size:
-        return pltpu.roll(values, step, axis)
-    upper = (lax.broadcasted_iota(jnp.int32, (8, LANES), axis) & step) != 0
-    return jnp.where(upper, pltpu.roll(values, step, axis), pltpu.roll(values, size - step, axis))
+    step = sublane_step(bit)
+    if step == 4:
+        return pltpu.roll(values, step, 0)
+    return jnp.where(upper_half(bit) != 0, pltpu.roll(values, step, 0), pltpu.roll(values, 8 - step, 0))
 
 
 def tile_pairs(bit):
-    step = 1 << (5 if bit == 8 else bit)
+    step = 1 << (bit if bit < 5 else 5 if bit == 8 else bit - 9)
     return [(i, i + step) for i in range(TILES) if not i & step]
 
 
 def is_tile_bit(bit):
-    return bit < 5 or bit == 8
+    return bit < 5 or 8 <= bit <= 12
+
+
+def flip_blocks(ref):
+    for part in range(ref.shape[0] // LANES):
+        rows = slice(part * LANES, (part + 1) * LANES)
+        ref[rows, :] = ref[rows, :].T
 
 
 def word(position):
@@ -80,7 +95,8 @@
 
 
 def place(tile_index):
-    inside = lax.broadcasted_iota(jnp.int32, (8, LANES), 0) * 32 + lax.broadcasted_iota(jnp.int32, (8, LANES), 1) * 512
+    lane = lax.broadcasted_iota(jnp.int32, (8, LANES), 1)
+    inside = lax.broadcasted_iota(jnp.int32, (8, LANES), 0) * 32 + ((lane & 7) << 13) + ((lane >> 3) << 9)
     return inside + ((tile_index & 31) + ((tile_index >> 5) << 8))
 
 
@@ -96,8 +112,7 @@
             bits = bits | jnp.where(swap, word(position), 0)
         mask_ref[at] = bits
         return
-    axis, step = (0, 1 << (bit - 5)) if bit < 8 else (1, 1 << (bit - 9))
-    upper = -((lax.broadcasted_iota(jnp.int32, (8, LANES), axis) & step) // step)
+    upper = jnp.where(upper_half(bit) != 0, -1, 0)
     for part in range(2):
         bits = jnp.zeros((8, LANES), jnp.int32)
         for position in range(32):
@@ -128,13 +143,26 @@
             view[...] = jnp.where((bits & word(position)) != 0, partner(own, bit), own)
 
 
-def network(stage, backwards=False, before=None):
+def network(stage, ref, mask_ref, backwards=False, before=None):
     def one_level(count, carry):
         level = LEVELS - count if backwards else count + 1
+
+        def run(bits):
+            for bit in bits if backwards else reversed(bits):
+                pl.when(in_network(level, bit))(functools.partial(stage, ref, mask_ref, level, bit))
+
+        def flipped():
+            flip_blocks(ref)
+            run(range(9, LEVELS))
+            flip_blocks(ref)
+
         if before is not None:
             before(level)
-        for bit in range(LEVELS) if backwards else reversed(range(LEVELS)):
-            pl.when(in_network(level, bit))(functools.partial(stage, level, bit))
+        if backwards:
+            run(range(9))
+        pl.when(level > 9)(flipped)
+        if not backwards:
+            run(range(9))
         return carry
 
     lax.fori_loop(0, LEVELS, one_level, 0)
@@ -153,7 +181,7 @@
             at = place(index)
             tile(key_ref, index)[...] ^= -(((at >> level) ^ (at >> (level - 1))) & 1)
 
-    network(functools.partial(sort_stage, key_ref, mask_ref), before=turn)
+    network(sort_stage, key_ref, mask_ref, before=turn)
 
     half = key_ref.shape[0] // 2
     for h in range(2):
@@ -297,40 +325,55 @@
 
 
 def main_kernel(
-    bound_ref, tail_ref, pix_ref, weight_ref, mask_ref, full_ref, form_ref, twist_ref, filt_ref, out_ref, tab_ref, series_ref, wide_ref
+    bound_ref, tail_ref, here_ref, pix_ref, weight_ref, mask_ref, mine_ref, peer_ref, form_ref, twist_ref, filt_ref, keep_ref, send_ref, *scratch
 ):
-    share_rows = full_ref.shape[1] // 3
-    map_rows = full_ref.shape[0] * share_rows
-
-    def lay(couple, carry):
-        row = pl.multiple_of(couple * 2 * share_rows, 8)
-        for comp in range(3):
-            parts = [full_ref[2 * couple + h, comp * share_rows : (comp + 1) * share_rows, :] for h in range(2)]
-            tab_ref[comp, pl.ds(row, 2 * share_rows), :] = jnp.concatenate(parts, axis=0)
+    tab_ref, series_ref, wide_ref = scratch
+    n_row = 4
+    plane = mine_ref.shape[0]
+    per_share = mine_ref.shape[1] // n_row
+    share_rows = per_share // 3
+    map_rows = plane * n_row * 2 * share_rows
+    upper_core = here_ref[1] != 0
+
+    def lay(spot, carry):
+        for back in range(n_row):
+            chip = ((here_ref[0] + (n_row - back)) & (n_row - 1)) * plane + spot
+            row = pl.multiple_of(chip * 2 * share_rows, 8)
+            for comp in range(3):
+                piece = slice(back * per_share + comp * share_rows, back * per_share + (comp + 1) * share_rows)
+                mine, peer = mine_ref[spot, piece, :], peer_ref[spot, piece, :]
+                both = [jnp.where(upper_core, peer, mine), jnp.where(upper_core, mine, peer)]
+                tab_ref[comp, pl.ds(row, 2 * share_rows), :] = jnp.concatenate(both, axis=0)
         return carry
 
-    lax.fori_loop(0, full_ref.shape[0] // 2, lay, 0)
+    lax.fori_loop(0, plane, lay, 0)
     tab_ref[:, map_rows:, :] = jnp.zeros((3, tab_ref.shape[1] - map_rows, LANES), jnp.float32)
 
     gather_all(bound_ref, pix_ref, weight_ref, tab_ref, wide_ref)
     for part in range(4):
         series_ref[part * LANES : (part + 1) * LANES, :] = wide_ref[:, part * LANES : (part + 1) * LANES].T
-    network(functools.partial(replay_stage, series_ref, mask_ref), backwards=True)
+    network(replay_stage, series_ref, mask_ref, backwards=True)
     filter_series(form_ref, twist_ref, filt_ref, tail_ref, series_ref)
-    network(functools.partial(replay_stage, series_ref, mask_ref))
+    network(replay_stage, series_ref, mask_ref)
     for part in range(4):
         wide_ref[:, part * LANES : (part + 1) * LANES] = series_ref[part * LANES : (part + 1) * LANES, :].T
     scatter_all(bound_ref, pix_ref, weight_ref, wide_ref, tab_ref)
 
-    def spread(chip, carry):
-        row = pl.multiple_of(chip * 2 * share_rows, 8)
-        for comp in range(3):
-            both = tab_ref[comp, pl.ds(row, 2 * share_rows), :]
-            for core in range(2):
-                out_ref[core, chip, comp * share_rows : (comp + 1) * share_rows, :] = both[core * share_rows : (core + 1) * share_rows]
+    def spread(couple, carry):
+        row = pl.multiple_of(couple * 4 * share_rows, 8)
+        sides = ([], [])
+        for chip in range(2):
+            for comp in range(3):
+                both = tab_ref[comp, pl.ds(row + chip * 2 * share_rows, 2 * share_rows), :]
+                low, high = both[:share_rows], both[share_rows:]
+                sides[0].append(jnp.where(upper_core, high, low))
+                sides[1].append(jnp.where(upper_core, low, high))
+        at = pl.multiple_of(couple * 2 * per_share, 8)
+        keep_ref[pl.ds(at, 2 * per_share), :] = jnp.concatenate(sides[0], axis=0)
+        send_ref[pl.ds(at, 2 * per_share), :] = jnp.concatenate(sides[1], axis=0)
         return carry
 
-    lax.fori_loop(0, out_ref.shape[1], spread, 0)
+    lax.fori_loop(0, plane * n_row // 2, spread, 0)
 
 
 def filter_tables(side):
@@ -391,12 +434,19 @@
     pointing = jnp.stack([a.reshape(det_rows, samples // LANES, LANES) for a in (pixels, angle_index, flag_mask)], axis=1)
     pointing = exchange(pointing, TM)
 
-    own = direction.reshape(1, 3 * share_rows, LANES)
-    full = exchange(jnp.broadcast_to(own, (n_dev, 3 * share_rows, LANES)), DET_TM)
+    own = direction.reshape(3 * share_rows, LANES)
+    n_row = lax.axis_size(ROW)
+    parts = [own] + [lax.ppermute(own, ROW, [(j, (j + s) % n_row) for j in range(n_row)]) for s in range(1, n_row)]
+    n_plane = lax.axis_size(PLANE)
+    spread = jnp.broadcast_to(jnp.concatenate(parts)[None], (n_plane, n_row * 3 * share_rows, LANES))
+    spread, pointing = lax.optimization_barrier((spread, pointing))
+    mine = exchange(spread, PLANE)
+    peer = lax.ppermute(mine, CORE, [(0, 1), (1, 0)])
+    here = jnp.stack([lax.axis_index(ROW), lax.axis_index(CORE)]).astype(jnp.int32)
 
     trig = jnp.stack([jnp.cos(2.0 * angles), jnp.sin(2.0 * angles)])
     wide = (LANES, total // LANES)
-    pix, weights, bounds, masks = pl.pallas_call(
+    ordering = pl.pallas_call(
         sort_kernel,
         in_specs=[VMEM, VMEM],
         out_specs=[VMEM] * 4,
@@ -407,20 +457,22 @@
             jax.ShapeDtypeStruct((SLOTS, 8, LANES), jnp.int32),
         ],
         scratch_shapes=[pltpu.VMEM((total // LANES, LANES), jnp.int32)],
-    )(pointing, trig)
+    )
+    pix, weights, bounds, masks = ordering(pointing, trig)
 
     doubled = inv_noise[0, : total // 2].reshape(side // 2, side).T * 2.0
     corner = jnp.zeros((side, side // 2), jnp.bool_).at[0, 0].set(True)
     doubled = jnp.where(corner, inv_noise[0, 0], doubled)
-    shares = pl.pallas_call(
+    halved = jax.ShapeDtypeStruct((n_dev // 2 * 3 * share_rows, LANES), f32)
+    keep, send = pl.pallas_call(
         main_kernel,
-        in_specs=[SMEM, SMEM] + [VMEM] * 7,
-        out_specs=VMEM,
-        out_shape=jax.ShapeDtypeStruct((2, n_dev // 2, 3 * share_rows, LANES), f32),
+        in_specs=[SMEM] * 3 + [VMEM] * 8,
+        out_specs=[VMEM] * 2,
+        out_shape=[halved] * 2,
         scratch_shapes=[pltpu.VMEM((3, map_rows + 8, LANES), f32), pltpu.VMEM((total // LANES, LANES), f32), pltpu.VMEM(wide, f32)],
-    )(bounds, inv_noise[0, total // 2 :], pix, weights, masks, full, forms, twists, doubled)
-
-    shares = jnp.sum(exchange(shares, CORE), axis=0)
+    )(bounds, inv_noise[0, total // 2 :], here, pix, weights, masks, mine, peer, forms, twists, doubled)
+
+    shares = (keep + lax.ppermute(send, CORE, [(0, 1), (1, 0)])).reshape(n_dev // 2, 3 * share_rows, LANES)
     image = jnp.sum(exchange(shares, CHIPS), axis=0).reshape(3, share_len)
 
     scaled_resid = precond * resid_map

time: 173 us -> 156 us (0.902)
  waiting for transfers between devices: 31.4 us -> 13.5 us
  blocking collectives: 46 us -> 63.1 us
  Pallas kernels: 54.2 us -> 44 us
  local copies, waits for them, and re-layouts: 11.1 us -> 5.91 us
    all_to_all x2 -> x1, waiting for transfers between devices: 31.4 us -> 6.99 us  [exchange(): return lax.all_to_all(array, axes, split_axis=0, concat_axis=0, tiled=True)]
    all_to_all x3, blocking collectives: 46 us -> 63.1 us  [exchange(): return lax.all_to_all(array, axes, split_axis=0, concat_axis=0, tiled=True)]
    pallas_call x2, Pallas kernels: 54.2 us -> 44 us  [the longest x1 32.4 us: body(): pl.pallas_call(main_kernel, in_specs=[SMEM] * 3 + [VMEM] * 8, out_specs=[...]
    ppermute x0 -> x5, waiting for transfers between devices: none -> 6.52 us  [the longest x3 3.53 us: body(): lax.ppermute(own, ROW, [(j, (j + s) % n_row) for j in range(n_row)])]
    all_to_all x2 -> x1, starting transfers between devices: 15.3 us -> 9.59 us  [exchange(): return lax.all_to_all(array, axes, split_axis=0, concat_axis=0, tiled=True)]
    ppermute x0 -> x5, starting transfers between devices: none -> 4.74 us  [the longest x3 3.67 us: body(): lax.ppermute(own, ROW, [(j, (j + s) % n_row) for j in range(n_row)])]
    pallas_call x1 -> x0, local copies, waits for them, and re-layouts: 2.2 us -> none  [body(): pl.pallas_call(main_kernel, in_specs=[SMEM, SMEM] + [VMEM] * 7, out_specs...]
    unnamed x21 -> x25, local copies, waits for them, and re-layouts: 4.55 us -> 3.77 us
  transfers between devices with their start and end apart: 2 -> 6, of which waited for: 2 -> 4; matrix products, arithmetic and copies ran while one was open for 2% -> 2% of each run, Pallas kernels for 9% -> 8%
where the time goes in v1:
time: 156 us; the launch traced here: 155 us
  blocking collectives  63.1 us (40%)
  Pallas kernels  44 us (28%)
  starting transfers between devices  14.3 us (9%)
  waiting for transfers between devices  13.5 us (9%)
  other arithmetic  8.73 us (6%)
  local copies, waits for them, and re-layouts  5.91 us (4%)
  between operations  5.88 us (4%)
    all_to_all x3, blocking collectives, exchange(): return lax.all_to_all(array, axes, split_axis=0, concat_axis=0, tiled=True)  63.1 us
    pallas_call x1, Pallas kernels, body(): pl.pallas_call(main_kernel, in_specs=[SMEM] * 3 + [VMEM] * 8, out_specs=[...  32.4 us
    pallas_call x1, Pallas kernels, body(): pix, weights, bounds, masks = ordering(pointing, trig)  11.7 us
    all_to_all x1, starting transfers between devices, exchange(): return lax.all_to_all(array, axes, split_axis=0, concat_axis=0, tiled=True)  9.59 us
    all_to_all x1, waiting for transfers between devices, exchange(): return lax.all_to_all(array, axes, split_axis=0, concat_axis=0, tiled=True)  6.99 us
    unnamed x25, local copies, waits for them, and re-layouts  3.77 us
    ppermute x3, starting transfers between devices, body(): lax.ppermute(own, ROW, [(j, (j + s) % n_row) for j in range(n_row)])  3.67 us
    ppermute x3, waiting for transfers between devices, body(): lax.ppermute(own, ROW, [(j, (j + s) % n_row) for j in range(n_row)])  3.53 us
  transfers between devices with their start and end apart: 6, of which 4 were waited for; matrix products, arithmetic and copies ran while one was open for 2% of the time, Pallas kernels for 8%

profile of v1, /device:TPU:1, one launch (start us, length us, event | category | flops | bytes accessed | tf_op | source)
XLA Modules:
  0.0 155.5 jit_solution(11755117126382630192)
XLA Ops:
  0.6 0.0 copy-start.3
  0.6 1.0 copy.19
  1.7 1.0 copy.20
  2.7 0.0 copy-done.3
  2.8 0.0 copy-start.4
  2.8 0.9 pad_add_fusion
  3.7 9.6 %all-to-all-start = ((s32[32,3,16,128]{3,2,1,0:T(8,128)}), s32[32,3,16,128]{3,2,1,0:T(8,128)S(1)}, u32[]{:S(2)}, u32[]{:S(2)}) async-start(s32[32,3,16,128]{3,2,1,0:T(8,128)} %pad_add_fusion), calls=%async_computation | async-start | bytes 1572864 | tf_op jit(solution)/shard_map/all_to_all | solution.py:29
  13.3 0.0 copy-done.4
  13.3 2.5 %collective-permute-start.2 = (f32[36,128]{1,0:T(8,128)S(1)}, f32[36,128]{1,0:T(8,128)S(1)}, u32[]{:S(2)}, u32[]{:S(2)}) collective-permute-start(f32[36,128]{1,0:T(8,128)S(1)} %reshape.57), channel_id=1, source_target_pairs={{0,96},{32,0},{64,32},{96,64},{1,97},{33,1},{65,33},{97,65},{2,98}... | collective-permute-start | bytes 55304 | tf_op jit(solution)/shard_map/ppermute | solution.py:439
  15.9 0.5 collective-permute-start.1
  16.4 0.6 collective-permute-start
  17.0 0.0 collective-permute-done.2
  17.0 3.3 %collective-permute-done.1 = f32[36,128]{1,0:T(8,128)S(1)} collective-permute-done((f32[36,128]{1,0:T(8,128)S(1)}, f32[36,128]{1,0:T(8,128)S(1)}, u32[]{:S(2)}, u32[]{:S(2)}) %collective-permute-start.1) | collective-permute-done | bytes 18464 | tf_op jit(solution)/shard_map/ppermute | solution.py:439
  20.3 0.2 collective-permute-done
  20.6 7.0 %all-to-all-done.pointing_ref = s32[32,3,16,128]{3,2,1,0:T(8,128)S(1)} async-done(((s32[32,3,16,128]{3,2,1,0:T(8,128)}), s32[32,3,16,128]{3,2,1,0:T(8,128)S(1)}, u32[]{:S(2)}, u32[]{:S(2)}) %all-to-all-start) | async-done | bytes 786464 | tf_op jit(solution)/shard_map/all_to_all | solution.py:29
  27.5 0.1 broadcast_in_dim.8
  27.6 0.0 copy-start.5
  27.6 0.0 copy-start.6
  27.7 0.0 copy-start.10
  27.7 21.9 %all_to_all.20.mine_ref = f32[16,144,128]{2,1,0:T(8,128)S(1)} all-to-all(f32[16,144,128]{2,1,0:T(8,128)S(1)} %broadcast_in_dim.8), channel_id=1, replica_groups=mesh['det'=4,'tm_0'=4,'tm_1'=4,'tm_2'=2] {'tm_0','tm_1'}, dimensions={0} | all-to-all | bytes 2359296 | tf_op jit(solution)/shard_map/all_to_all | solution.py:29
  49.5 0.0 copy-done.1
  49.5 1.0 collective-permute-start.3
  50.5 0.0 copy-done.5
  50.5 0.5 fusion.1
  51.0 0.0 copy-done.6
  51.0 1.1 select_reduce_fusion
  52.2 0.8 copy.17
  53.0 0.6 pad_add_fusion.1.here_ref
  53.6 0.0 copy-done.10
  53.6 0.6 pad_maximum_fusion.1.trig_ref
  54.2 11.7 %shard_map.138 = (s32[128,512]{1,0:T(8,128)}, f32[3,128,512]{2,1,0:T(8,128)}, s32[4,128]{1,0:T(4,128)}, s32[272,8,128]{2,1,0:T(8,128)}) custom-call(s32[32,3,16,128]{3,2,1,0:T(8,128)} %copy-done.1, f32[2,128]{1,0:T(2,128)} %pad_maximum_fusion.1.trig_ref), custom_call_target="tpu_custom_call" | custom-call | tf_op jit(solution)/shard_map/pallas_call | solution.py:461
  65.8 0.0 collective-permute-done.3.peer_ref
  65.8 0.0 copy-done
  65.9 1.0 copy-done.2
  66.9 32.4 %shard_map.139 = (f32[2304,128]{1,0:T(8,128)}, f32[2304,128]{1,0:T(8,128)}) custom-call(s32[4,128]{1,0:T(4,128)} %get-tuple-element.25.bound_ref, f32[1]{0:T(128)} %bitcast.3.tail_ref, s32[2]{0:T(128)} %pad_add_fusion.1.here_ref, s32[128,512]{1,0:T(8,128)} %get-tuple-element.26.pix_ref, f32[3,128,512]{2,1,0:T(8,128)} %get-tuple-element.27.weight_ref, ...), custom_call_target="tpu_custom_call" | custom-call | tf_op jit(solution)/shard_map/pallas_call | solution.py:467
  99.3 0.1 collective-permute-start.4
  99.3 3.0 %collective-permute-done.4 = f32[2304,128]{1,0:T(8,128)S(1)} collective-permute-done((f32[2304,128]{1,0:T(8,128)}, f32[2304,128]{1,0:T(8,128)S(1)}, u32[]{:S(2)}, u32[]{:S(2)}) %collective-permute-start.4) | collective-permute-done | bytes 1179680 | tf_op jit(solution)/shard_map/ppermute | solution.py:475
  102.3 1.4 add.16
  103.7 0.1 reshape.58
  103.8 26.1 %all_to_all.21 = f32[64,36,128]{2,1,0:T(8,128)S(1)} all-to-all(f32[64,36,128]{2,1,0:T(8,128)S(1)} %reshape.58), channel_id=1, replica_groups=mesh['det'=4,'tm_0'=4,'tm_1'=4,'tm_2'=2] {'det','tm_0','tm_1'}, dimensions={0} | all-to-all | bytes 2359296 | tf_op jit(solution)/shard_map/all_to_all | solution.py:29
  129.9 0.1 reduce_sum.55
  130.0 0.6 copy-done.7
  130.6 0.0 copy-done.8
  130.6 0.6 multiply_reduce_fusion.2
  131.3 2.7 %select_maximum_fusion = f32[128]{0:T(128)S(1)} fusion(f32[1]{0:T(128)} %bitcast.10, f32[1]{0:T(128)} %bitcast.9, f32[1]{0:T(128)} %bitcast.8, f32[1]{0:T(128)} %bitcast), kind=kLoop, calls=%fused_computation.12 | loop fusion | flops 1024 | bytes 528 | tf_op jit(solution)/shard_map/stack | solution.py:479
  134.0 15.1 %all_to_all.22 = f32[128,1,128]{2,1,0:T(1,128)S(1)} all-to-all(f32[128,1,128]{2,1,0:T(1,128)S(1)} %broadcast_in_dim.18), channel_id=1, replica_groups=mesh['det'=4,'tm_0'=4,'tm_1'=4,'tm_2'=2] {'det','tm_0','tm_1','tm_2'}, dimensions={0} | all-to-all | bytes 131072 | tf_op jit(solution)/shard_map/all_to_all | solution.py:29
  149.1 0.6 fusion.2
  153.7 0.6 multiply_add_fusion
  (15 shorter events, 0.3 us)
Async XLA Ops:
  0.6 2.1 %copy-start.3 = (s32[32,2048]{1,0:T(8,128)S(1)}, s32[32,2048]{1,0:T(8,128)}, u32[]{:S(2)}) copy-start(s32[32,2048]{1,0:T(8,128)} %param.20) | copy-start | bytes 786436
  2.8 10.6 %copy-start.4 = (f32[3,1536]{1,0:T(4,128)S(1)}, f32[3,1536]{1,0:T(4,128)}, u32[]{:S(2)}) copy-start(f32[3,1536]{1,0:T(4,128)} %param.15) | copy-start | bytes 55300
  3.7 23.8 %all-to-all-start = ((s32[32,3,16,128]{3,2,1,0:T(8,128)}), s32[32,3,16,128]{3,2,1,0:T(8,128)S(1)}, u32[]{:S(2)}, u32[]{:S(2)}) async-start(s32[32,3,16,128]{3,2,1,0:T(8,128)} %pad_add_fusion), calls=%async_computation | async-start | bytes 1572864 | tf_op jit(solution)/shard_map/all_to_all | solution.py:29
  13.3 3.7 %collective-permute-start.2 = (f32[36,128]{1,0:T(8,128)S(1)}, f32[36,128]{1,0:T(8,128)S(1)}, u32[]{:S(2)}, u32[]{:S(2)}) collective-permute-start(f32[36,128]{1,0:T(8,128)S(1)} %reshape.57), channel_id=1, source_target_pairs={{0,96},{32,0},{64,32},{96,64},{1,97},{33,1},{65,33},{97,65},{2,98}... | collective-permute-start | bytes 55304 | tf_op jit(solution)/shard_map/ppermute | solution.py:439
  15.9 4.4 %collective-permute-start.1 = (f32[36,128]{1,0:T(8,128)S(1)}, f32[36,128]{1,0:T(8,128)S(1)}, u32[]{:S(2)}, u32[]{:S(2)}) collective-permute-start(f32[36,128]{1,0:T(8,128)S(1)} %reshape.57), channel_id=1, source_target_pairs={{0,64},{32,96},{64,0},{96,32},{1,65},{33,97},{65,1},{97,33},{2,66}... | collective-permute-start | bytes 55304 | tf_op jit(solution)/shard_map/ppermute | solution.py:439
  16.4 4.1 %collective-permute-start = (f32[36,128]{1,0:T(8,128)S(1)}, f32[36,128]{1,0:T(8,128)S(1)}, u32[]{:S(2)}, u32[]{:S(2)}) collective-permute-start(f32[36,128]{1,0:T(8,128)S(1)} %reshape.57), channel_id=1, source_target_pairs={{0,32},{32,64},{64,96},{96,0},{1,33},{33,65},{65,97},{97,1},{2,34}... | collective-permute-start | bytes 55304 | tf_op jit(solution)/shard_map/ppermute | solution.py:439
  27.5 22.0 %copy-start.1 = (s32[32,3,16,128]{3,2,1,0:T(8,128)}, s32[32,3,16,128]{3,2,1,0:T(8,128)S(1)}, u32[]{:S(2)}) copy-start(s32[32,3,16,128]{3,2,1,0:T(8,128)S(1)} %all-to-all-done.pointing_ref) | copy-start | bytes 2359300
  27.6 22.9 %copy-start.5 = (f32[1,32769]{1,0:T(1,128)S(1)}, f32[1,32769]{1,0:T(1,128)}, u32[]{:S(2)}) copy-start(f32[1,32769]{1,0:T(1,128)} %param.21) | copy-start | bytes 393232
  27.6 23.4 %copy-start.6 = (pred[1,32768]{1,0:T(4,128)(4,1)S(1)}, pred[1,32768]{1,0:T(4,128)(4,1)}, u32[]{:S(2)}) copy-start(pred[1,32768]{1,0:T(4,128)(4,1)} %constant.56.clone.1) | copy-start | bytes 98308
  27.7 25.9 %copy-start.10 = (f32[128]{0:T(128)S(1)}, f32[128]{0:T(128)}, u32[]{:S(2)}) copy-start(f32[128]{0:T(128)} %param.19) | copy-start | bytes 1540
  49.5 16.3 %copy-start = (f32[16,144,128]{2,1,0:T(8,128)}, f32[16,144,128]{2,1,0:T(8,128)S(1)}, u32[]{:S(2)}) copy-start(f32[16,144,128]{2,1,0:T(8,128)S(1)} %all_to_all.20.mine_ref) | copy-start | bytes 3538948
  49.5 16.3 %collective-permute-start.3 = (f32[16,144,128]{2,1,0:T(8,128)S(1)}, f32[16,144,128]{2,1,0:T(8,128)S(1)}, u32[]{:S(2)}, u32[]{:S(2)}) collective-permute-start(f32[16,144,128]{2,1,0:T(8,128)S(1)} %all_to_all.20.mine_ref), channel_id=1, source_target_pairs={{0,1},{1,0},{2,3},{3,2},{4,5},{5,4},{6,7},{7,6},{8,9},{9,8},{10,11... | collective-permute-start | bytes 3538952 | tf_op jit(solution)/shard_map/ppermute | solution.py:444
  65.8 1.0 copy-start.2
  99.3 3.1 %collective-permute-start.4 = (f32[2304,128]{1,0:T(8,128)}, f32[2304,128]{1,0:T(8,128)S(1)}, u32[]{:S(2)}, u32[]{:S(2)}) collective-permute-start(f32[2304,128]{1,0:T(8,128)} %get-tuple-element.31), channel_id=1, source_target_pairs={{0,1},{1,0},{2,3},{3,2},{4,5},{5,4},{6,7},{7,6},{8,9},{9,8},{10,11... | collective-permute-start | bytes 3538952 | tf_op jit(solution)/shard_map/ppermute | solution.py:475
  129.9 0.7 copy-start.7
  129.9 0.8 copy-start.8
  129.9 23.8 %copy-start.9 = (f32[3,1536]{1,0:T(4,128)S(1)}, f32[3,1536]{1,0:T(4,128)}, u32[]{:S(2)}) copy-start(f32[3,1536]{1,0:T(4,128)} %param.13) | copy-start | bytes 55300

commit v2 on v1

--- a/solution.py
+++ b/solution.py
@@ -420,6 +420,42 @@
     x_ref[pl.ds(1, side, 2), :] = result[:, half:]
 
 
+def sums_kernel(shares_ref, resid_ref, direction_ref, precond_ref, image_ref, sums_ref):
+    rows = jnp.sum(shares_ref[...], axis=0)
+    share_rows = rows.shape[0] * rows.shape[1] // 3
+    for comp in range(3):
+        for j in range(share_rows):
+            at = comp * share_rows + j
+            image_ref[comp : comp + 1, j * LANES : (j + 1) * LANES] = rows[at // 4, at % 4 : at % 4 + 1]
+    image = image_ref[...]
+    scaled = precond_ref[...] * resid_ref[...]
+    group = lax.broadcasted_iota(jnp.int32, (1, LANES), 1) >> 5
+    merged = jnp.zeros((1, LANES), jnp.float32)
+    for index, terms in enumerate((scaled * resid_ref[...], direction_ref[...] * image, image * scaled, image * precond_ref[...] * image)):
+        row = jnp.sum(terms, axis=0, keepdims=True)
+        row = functools.reduce(jnp.add, [row[:, j * LANES : (j + 1) * LANES] for j in range(share_rows)])
+        row = row + pltpu.roll(row, 64, 1)
+        row = row + pltpu.roll(row, 32, 1)
+        merged = jnp.where(group == index, row, merged)
+    sums_ref[...] = jnp.broadcast_to(merged.reshape(1, 1, LANES), sums_ref.shape)
+
+
+def update_kernel(sums_ref, image_ref, sol_ref, resid_ref, direction_ref, precond_ref, new_sol_ref, new_resid_ref, new_dir_ref, norm_ref):
+    row = jnp.sum(sums_ref[...], axis=0)
+    group = lax.broadcasted_iota(jnp.int32, (1, LANES), 1) >> 5
+    norm_old, curvature, cross_term, image_norm = (
+        jnp.sum(jnp.where(group == index, row, 0.0), axis=1, keepdims=True) for index in range(4)
+    )
+    step_size = norm_old / curvature
+    new_norm = norm_old - 2.0 * step_size * cross_term + step_size * step_size * image_norm
+    direction = direction_ref[...]
+    new_resid = resid_ref[...] - step_size * image_ref[...]
+    new_resid_ref[...] = new_resid
+    new_sol_ref[...] = sol_ref[...] + step_size * direction
+    new_dir_ref[...] = precond_ref[...] * new_resid + (new_norm / norm_old) * direction
+    norm_ref[...] = new_norm
+
+
 def body(sol_map, resid_map, direction, precond, pixels, angle_index, angles, flag_mask, inv_noise, forms, twists):
     share_len = direction.shape[1]
     n_dev = lax.axis_size(DET_TM)
@@ -472,27 +508,15 @@
         scratch_shapes=[pltpu.VMEM((3, map_rows + 8, LANES), f32), pltpu.VMEM((total // LANES, LANES), f32), pltpu.VMEM(wide, f32)],
     )(bounds, inv_noise[0, total // 2 :], here, pix, weights, masks, mine, peer, forms, twists, doubled)
 
-    shares = (keep + lax.ppermute(send, CORE, [(0, 1), (1, 0)])).reshape(n_dev // 2, 3 * share_rows, LANES)
-    image = jnp.sum(exchange(shares, CHIPS), axis=0).reshape(3, share_len)
-
-    scaled_resid = precond * resid_map
-    scalars = jnp.stack(
-        [
-            jnp.sum(scaled_resid * resid_map),
-            jnp.sum(direction * image),
-            jnp.sum(image * scaled_resid),
-            jnp.sum(image * precond * image),
-        ]
-    )
-    scalars = jnp.pad(scalars, (0, LANES - 4)).reshape(1, 1, LANES)
-    scalars = jnp.sum(exchange(jnp.broadcast_to(scalars, (n_dev, 1, LANES)), DET_TM), axis=(0, 1))
-    norm_old, curvature, cross_term, image_norm = scalars[0], scalars[1], scalars[2], scalars[3]
-    step_size = norm_old / curvature
-    new_resid = resid_map - step_size * image
-    new_norm = norm_old - 2.0 * step_size * cross_term + step_size * step_size * image_norm
-    new_sol = sol_map + step_size * direction
-    new_dir = precond * new_resid + new_norm / norm_old * direction
-    return (new_sol, new_resid, new_dir, new_norm)
+    shares = (keep + lax.ppermute(send, CORE, [(0, 1), (1, 0)])).reshape(n_dev // 2, 3 * share_rows // 4, 4, LANES)
+    own_map = jax.ShapeDtypeStruct((3, share_len), f32)
+    image, sums = pl.pallas_call(
+        sums_kernel, in_specs=[VMEM] * 4, out_specs=[VMEM] * 2, out_shape=[own_map, jax.ShapeDtypeStruct((n_dev, 1, LANES), f32)]
+    )(exchange(shares, CHIPS), resid_map, direction, precond)
+    new_sol, new_resid, new_dir, new_norm = pl.pallas_call(
+        update_kernel, in_specs=[VMEM] * 6, out_specs=[VMEM] * 4, out_shape=[own_map] * 3 + [jax.ShapeDtypeStruct((1, 1), f32)]
+    )(exchange(sums, DET_TM), image, sol_map, resid_map, direction, precond)
+    return (new_sol, new_resid, new_dir, new_norm.reshape(()))
 
 
 def solution(mesh):

time: 156 us -> 150 us (0.962)
  between operations: 5.88 us -> 0.76 us
  Pallas kernels: 44 us -> 48.1 us
  other arithmetic: 8.73 us -> 4.65 us
    pallas_call x0 -> x2, Pallas kernels: none -> 4.07 us  [the longest x1 2.34 us: body(): pl.pallas_call(sums_kernel, in_specs=[VMEM] * 4, out_specs=[VMEM] * 2, ou...]
    another operation x1 -> x0, other arithmetic: 2.66 us -> none  [body(): jnp.stack([jnp.sum(scaled_resid * resid_map), jnp.sum(direction * image),...]
    unnamed x25 -> x19, local copies, waits for them, and re-layouts: 3.77 us -> 3.13 us
where the time goes in v2:
time: 150 us; the launch traced here: 149 us
  blocking collectives  63.4 us (42%)
  Pallas kernels  48.1 us (32%)
  starting transfers between devices  14.3 us (10%)
  waiting for transfers between devices  13.5 us (9%)
  other arithmetic  4.65 us (3%)
  local copies, waits for them, and re-layouts  4.55 us (3%)
    all_to_all x3, blocking collectives, exchange(): return lax.all_to_all(array, axes, split_axis=0, concat_axis=0, tiled=True)  63.4 us
    pallas_call x1, Pallas kernels, body(): pl.pallas_call(main_kernel, in_specs=[SMEM] * 3 + [VMEM] * 8, out_specs=[...  32.4 us
    pallas_call x1, Pallas kernels, body(): pix, weights, bounds, masks = ordering(pointing, trig)  11.7 us
    all_to_all x1, starting transfers between devices, exchange(): return lax.all_to_all(array, axes, split_axis=0, concat_axis=0, tiled=True)  9.59 us
    all_to_all x1, waiting for transfers between devices, exchange(): return lax.all_to_all(array, axes, split_axis=0, concat_axis=0, tiled=True)  6.99 us
    ppermute x3, starting transfers between devices, body(): lax.ppermute(own, ROW, [(j, (j + s) % n_row) for j in range(n_row)])  3.67 us
    ppermute x3, waiting for transfers between devices, body(): lax.ppermute(own, ROW, [(j, (j + s) % n_row) for j in range(n_row)])  3.53 us
    unnamed x19, local copies, waits for them, and re-layouts  3.13 us
  transfers between devices with their start and end apart: 6, of which 4 were waited for; matrix products, arithmetic and copies ran while one was open for 2% of the time, Pallas kernels for 8%

profile of v2, /device:TPU:1, one launch (start us, length us, event | category | flops | bytes accessed | tf_op | source)
XLA Modules:
  0.0 149.3 jit_solution(20387873772963817)
XLA Ops:
  0.6 0.0 copy-start.3
  0.6 1.0 copy.16
  1.7 1.0 copy.17
  2.7 0.0 copy-done.3
  2.8 0.0 copy-start.4
  2.8 0.9 pad_add_fusion
  3.7 9.6 %all-to-all-start = ((s32[32,3,16,128]{3,2,1,0:T(8,128)}), s32[32,3,16,128]{3,2,1,0:T(8,128)S(1)}, u32[]{:S(2)}, u32[]{:S(2)}) async-start(s32[32,3,16,128]{3,2,1,0:T(8,128)} %pad_add_fusion), calls=%async_computation | async-start | bytes 1572864 | tf_op jit(solution)/shard_map/all_to_all | solution.py:29
  13.3 0.0 copy-done.4
  13.3 2.5 %collective-permute-start.2 = (f32[36,128]{1,0:T(8,128)S(1)}, f32[36,128]{1,0:T(8,128)S(1)}, u32[]{:S(2)}, u32[]{:S(2)}) collective-permute-start(f32[36,128]{1,0:T(8,128)S(1)} %reshape.53), channel_id=1, source_target_pairs={{0,96},{32,0},{64,32},{96,64},{1,97},{33,1},{65,33},{97,65},{2,98}... | collective-permute-start | bytes 55304 | tf_op jit(solution)/shard_map/ppermute | solution.py:475
  15.9 0.5 collective-permute-start.1
  16.4 0.6 collective-permute-start
  17.0 0.0 collective-permute-done.2
  17.0 3.3 %collective-permute-done.1 = f32[36,128]{1,0:T(8,128)S(1)} collective-permute-done((f32[36,128]{1,0:T(8,128)S(1)}, f32[36,128]{1,0:T(8,128)S(1)}, u32[]{:S(2)}, u32[]{:S(2)}) %collective-permute-start.1) | collective-permute-done | bytes 18464 | tf_op jit(solution)/shard_map/ppermute | solution.py:475
  20.3 0.2 collective-permute-done
  20.6 7.0 %all-to-all-done.pointing_ref = s32[32,3,16,128]{3,2,1,0:T(8,128)S(1)} async-done(((s32[32,3,16,128]{3,2,1,0:T(8,128)}), s32[32,3,16,128]{3,2,1,0:T(8,128)S(1)}, u32[]{:S(2)}, u32[]{:S(2)}) %all-to-all-start) | async-done | bytes 786464 | tf_op jit(solution)/shard_map/all_to_all | solution.py:29
  27.5 0.0 copy-start.1
  27.6 0.1 broadcast_in_dim.5
  27.6 0.0 copy-start.5
  27.6 0.0 copy-start.6
  27.7 0.0 copy-start.7
  27.7 21.9 %all_to_all.20.mine_ref = f32[16,144,128]{2,1,0:T(8,128)S(1)} all-to-all(f32[16,144,128]{2,1,0:T(8,128)S(1)} %broadcast_in_dim.5), channel_id=1, replica_groups=mesh['det'=4,'tm_0'=4,'tm_1'=4,'tm_2'=2] {'tm_0','tm_1'}, dimensions={0} | all-to-all | bytes 2359296 | tf_op jit(solution)/shard_map/all_to_all | solution.py:29
  49.5 0.0 copy-done.1
  49.5 0.0 copy-start
  49.5 1.0 collective-permute-start.3
  50.5 0.0 copy-done.5
  50.5 0.5 fusion
  51.1 0.0 copy-done.6
  51.1 1.1 select_reduce_fusion
  52.2 0.8 copy.15
  53.0 0.6 pad_add_fusion.1.here_ref
  53.6 0.0 copy-done.7
  53.6 0.6 pad_maximum_fusion.1.trig_ref
  54.2 11.7 %shard_map.138 = (s32[128,512]{1,0:T(8,128)}, f32[3,128,512]{2,1,0:T(8,128)}, s32[4,128]{1,0:T(4,128)}, s32[272,8,128]{2,1,0:T(8,128)}) custom-call(s32[32,3,16,128]{3,2,1,0:T(8,128)} %copy-done.1, f32[2,128]{1,0:T(2,128)} %pad_maximum_fusion.1.trig_ref), custom_call_target="tpu_custom_call" | custom-call | tf_op jit(solution)/shard_map/pallas_call | solution.py:497
  65.9 0.0 collective-permute-done.3.peer_ref
  65.9 0.0 copy-start.2
  65.9 0.0 copy-done
  65.9 1.0 copy-done.2
  66.9 32.4 %shard_map.139 = (f32[2304,128]{1,0:T(8,128)}, f32[2304,128]{1,0:T(8,128)}) custom-call(s32[4,128]{1,0:T(4,128)} %get-tuple-element.31.bound_ref, f32[1]{0:T(128)} %bitcast.2.tail_ref, s32[2]{0:T(128)} %pad_add_fusion.1.here_ref, s32[128,512]{1,0:T(8,128)} %get-tuple-element.32.pix_ref, f32[3,128,512]{2,1,0:T(8,128)} %get-tuple-element.33.weight_ref, ...), custom_call_target="tpu_custom_call" | custom-call | tf_op jit(solution)/shard_map/pallas_call | solution.py:503
  99.3 0.1 collective-permute-start.4
  99.4 3.0 %collective-permute-done.4 = f32[2304,128]{1,0:T(8,128)S(1)} collective-permute-done((f32[2304,128]{1,0:T(8,128)}, f32[2304,128]{1,0:T(8,128)S(1)}, u32[]{:S(2)}, u32[]{:S(2)}) %collective-permute-start.4) | collective-permute-done | bytes 1179680 | tf_op jit(solution)/shard_map/ppermute | solution.py:511
  102.3 1.4 add.5
  103.7 24.9 %all_to_all.21.shares_ref = f32[64,9,4,128]{3,2,1,0:T(4,128)} all-to-all(f32[64,9,4,128]{3,2,1,0:T(4,128)S(1)} %bitcast.20), channel_id=1, replica_groups=mesh['det'=4,'tm_0'=4,'tm_1'=4,'tm_2'=2] {'det','tm_0','tm_1'}, dimensions={0} | all-to-all | bytes 2359296 | tf_op jit(solution)/shard_map/all_to_all | solution.py:29
  128.6 2.3 %shard_map.140 = (f32[3,1536]{1,0:T(4,128)}, f32[128,1,128]{2,1,0:T(1,128)}) custom-call(f32[64,9,4,128]{3,2,1,0:T(4,128)} %all_to_all.21.shares_ref, f32[3,1536]{1,0:T(4,128)} %resid_ref.3, f32[3,1536]{1,0:T(4,128)} %direction_ref.3, f32[3,1536]{1,0:T(4,128)} %precond_ref.3), custom_call_target="tpu_custom_call" | custom-call | tf_op jit(solution)/shard_map/pallas_call | solution.py:513
  131.0 16.6 %all_to_all.22.sums_ref = f32[128,1,128]{2,1,0:T(1,128)} all-to-all(f32[128,1,128]{2,1,0:T(1,128)} %get-tuple-element.38), channel_id=1, replica_groups=mesh['det'=4,'tm_0'=4,'tm_1'=4,'tm_2'=2] {'det','tm_0','tm_1','tm_2'}, dimensions={0} | all-to-all | bytes 131072 | tf_op jit(solution)/shard_map/all_to_all | solution.py:29
  147.6 1.7 %shard_map.141 = (f32[3,1536]{1,0:T(4,128)}, f32[3,1536]{1,0:T(4,128)}, f32[3,1536]{1,0:T(4,128)}, f32[1,1]{1,0:T(1,128)}) custom-call(f32[128,1,128]{2,1,0:T(1,128)} %all_to_all.22.sums_ref, f32[3,1536]{1,0:T(4,128)} %get-tuple-element.39.image_ref, f32[3,1536]{1,0:T(4,128)} %sol_ref.1, f32[3,1536]{1,0:T(4,128)} %resid_ref.3, f32[3,1536]{1,0:T(4,128)} %direction_ref.3, ...), custom_call_target="tpu_custom_call" | custom-call | tf_op jit(solution)/shard_map/pallas_call | solution.py:516
  (5 shorter events, 0.2 us)
Async XLA Ops:
  0.6 2.1 %copy-start.3 = (s32[32,2048]{1,0:T(8,128)S(1)}, s32[32,2048]{1,0:T(8,128)}, u32[]{:S(2)}) copy-start(s32[32,2048]{1,0:T(8,128)} %param.20) | copy-start | bytes 786436
  2.8 10.6 %copy-start.4 = (f32[3,1536]{1,0:T(4,128)S(1)}, f32[3,1536]{1,0:T(4,128)}, u32[]{:S(2)}) copy-start(f32[3,1536]{1,0:T(4,128)} %direction_ref.3) | copy-start | bytes 55300
  3.7 23.8 %all-to-all-start = ((s32[32,3,16,128]{3,2,1,0:T(8,128)}), s32[32,3,16,128]{3,2,1,0:T(8,128)S(1)}, u32[]{:S(2)}, u32[]{:S(2)}) async-start(s32[32,3,16,128]{3,2,1,0:T(8,128)} %pad_add_fusion), calls=%async_computation | async-start | bytes 1572864 | tf_op jit(solution)/shard_map/all_to_all | solution.py:29
  13.3 3.7 %collective-permute-start.2 = (f32[36,128]{1,0:T(8,128)S(1)}, f32[36,128]{1,0:T(8,128)S(1)}, u32[]{:S(2)}, u32[]{:S(2)}) collective-permute-start(f32[36,128]{1,0:T(8,128)S(1)} %reshape.53), channel_id=1, source_target_pairs={{0,96},{32,0},{64,32},{96,64},{1,97},{33,1},{65,33},{97,65},{2,98}... | collective-permute-start | bytes 55304 | tf_op jit(solution)/shard_map/ppermute | solution.py:475
  15.9 4.4 %collective-permute-start.1 = (f32[36,128]{1,0:T(8,128)S(1)}, f32[36,128]{1,0:T(8,128)S(1)}, u32[]{:S(2)}, u32[]{:S(2)}) collective-permute-start(f32[36,128]{1,0:T(8,128)S(1)} %reshape.53), channel_id=1, source_target_pairs={{0,64},{32,96},{64,0},{96,32},{1,65},{33,97},{65,1},{97,33},{2,66}... | collective-permute-start | bytes 55304 | tf_op jit(solution)/shard_map/ppermute | solution.py:475
  16.4 4.1 %collective-permute-start = (f32[36,128]{1,0:T(8,128)S(1)}, f32[36,128]{1,0:T(8,128)S(1)}, u32[]{:S(2)}, u32[]{:S(2)}) collective-permute-start(f32[36,128]{1,0:T(8,128)S(1)} %reshape.53), channel_id=1, source_target_pairs={{0,32},{32,64},{64,96},{96,0},{1,33},{33,65},{65,97},{97,1},{2,34}... | collective-permute-start | bytes 55304 | tf_op jit(solution)/shard_map/ppermute | solution.py:475
  27.5 22.0 %copy-start.1 = (s32[32,3,16,128]{3,2,1,0:T(8,128)}, s32[32,3,16,128]{3,2,1,0:T(8,128)S(1)}, u32[]{:S(2)}) copy-start(s32[32,3,16,128]{3,2,1,0:T(8,128)S(1)} %all-to-all-done.pointing_ref) | copy-start | bytes 2359300
  27.6 22.9 %copy-start.5 = (f32[1,32769]{1,0:T(1,128)S(1)}, f32[1,32769]{1,0:T(1,128)}, u32[]{:S(2)}) copy-start(f32[1,32769]{1,0:T(1,128)} %param.21) | copy-start | bytes 393232
  27.6 23.4 %copy-start.6 = (pred[1,32768]{1,0:T(4,128)(4,1)S(1)}, pred[1,32768]{1,0:T(4,128)(4,1)}, u32[]{:S(2)}) copy-start(pred[1,32768]{1,0:T(4,128)(4,1)} %constant.51.clone.1) | copy-start | bytes 98308
  27.7 25.9 %copy-start.7 = (f32[128]{0:T(128)S(1)}, f32[128]{0:T(128)}, u32[]{:S(2)}) copy-start(f32[128]{0:T(128)} %param.19) | copy-start | bytes 1540
  49.5 16.4 %copy-start = (f32[16,144,128]{2,1,0:T(8,128)}, f32[16,144,128]{2,1,0:T(8,128)S(1)}, u32[]{:S(2)}) copy-start(f32[16,144,128]{2,1,0:T(8,128)S(1)} %all_to_all.20.mine_ref) | copy-start | bytes 3538948
  49.5 16.4 %collective-permute-start.3 = (f32[16,144,128]{2,1,0:T(8,128)S(1)}, f32[16,144,128]{2,1,0:T(8,128)S(1)}, u32[]{:S(2)}, u32[]{:S(2)}) collective-permute-start(f32[16,144,128]{2,1,0:T(8,128)S(1)} %all_to_all.20.mine_ref), channel_id=1, source_target_pairs={{0,1},{1,0},{2,3},{3,2},{4,5},{5,4},{6,7},{7,6},{8,9},{9,8},{10,11... | collective-permute-start | bytes 3538952 | tf_op jit(solution)/shard_map/ppermute | solution.py:480
  65.9 1.0 copy-start.2
  99.3 3.1 %collective-permute-start.4 = (f32[2304,128]{1,0:T(8,128)}, f32[2304,128]{1,0:T(8,128)S(1)}, u32[]{:S(2)}, u32[]{:S(2)}) collective-permute-start(f32[2304,128]{1,0:T(8,128)} %get-tuple-element.37), channel_id=1, source_target_pairs={{0,1},{1,0},{2,3},{3,2},{4,5},{5,4},{6,7},{7,6},{8,9},{9,8},{10,11... | collective-permute-start | bytes 3538952 | tf_op jit(solution)/shard_map/ppermute | solution.py:511

commit v3 on v2

--- a/solution.py
+++ b/solution.py
@@ -20,7 +20,7 @@
 LANES = 128
 CHUNK = 256
 WINDOW = 16
-ROWS = 16
+ROWS = 32
 VMEM = pl.BlockSpec(memory_space=pltpu.VMEM)
 SMEM = pl.BlockSpec(memory_space=pltpu.SMEM)
 
@@ -420,6 +420,16 @@
     x_ref[pl.ds(1, side, 2), :] = result[:, half:]
 
 
+def message_kernel(pixels_ref, angle_ref, flag_ref, out_ref):
+    det_rows, samples = pixels_ref.shape
+    blocks = samples // LANES
+    for which, ref in enumerate((pixels_ref, angle_ref, flag_ref)):
+        for group in range(det_rows // 8):
+            for block in range(blocks):
+                at = group * 8 * 3 * blocks + which * blocks + block
+                out_ref[pl.ds(at, 8, 3 * blocks), :] = ref[group * 8 : group * 8 + 8, block * LANES : (block + 1) * LANES]
+
+
 def sums_kernel(shares_ref, resid_ref, direction_ref, precond_ref, image_ref, sums_ref):
     rows = jnp.sum(shares_ref[...], axis=0)
     share_rows = rows.shape[0] * rows.shape[1] // 3
@@ -467,14 +477,18 @@
     side = math.isqrt(total)
     f32 = jnp.float32
 
-    pointing = jnp.stack([a.reshape(det_rows, samples // LANES, LANES) for a in (pixels, angle_index, flag_mask)], axis=1)
+    blocks = samples // LANES
+    pointing = pl.pallas_call(
+        message_kernel, in_specs=[VMEM] * 3, out_specs=VMEM, out_shape=jax.ShapeDtypeStruct((det_rows * 3 * blocks, LANES), jnp.int32)
+    )(pixels, angle_index, flag_mask).reshape(det_rows, 3, blocks, LANES)
     pointing = exchange(pointing, TM)
 
     own = direction.reshape(3 * share_rows, LANES)
     n_row = lax.axis_size(ROW)
     parts = [own] + [lax.ppermute(own, ROW, [(j, (j + s) % n_row) for j in range(n_row)]) for s in range(1, n_row)]
     n_plane = lax.axis_size(PLANE)
-    spread = jnp.broadcast_to(jnp.concatenate(parts)[None], (n_plane, n_row * 3 * share_rows, LANES))
+    column = jnp.concatenate(parts)[None]
+    spread = jnp.broadcast_to(column, (n_plane, n_row * 3 * share_rows, LANES))
     spread, pointing = lax.optimization_barrier((spread, pointing))
     mine = exchange(spread, PLANE)
     peer = lax.ppermute(mine, CORE, [(0, 1), (1, 0)])

time: 150 us -> 148 us (0.987)
  local copies, waits for them, and re-layouts: 4.55 us -> 2.44 us
    pallas_call x0 -> x1, Pallas kernels: none -> 2.23 us  [body(): pl.pallas_call(message_kernel, in_specs=[VMEM] * 3, out_specs=VMEM, out_s...]
    unnamed x19 -> x14, local copies, waits for them, and re-layouts: 3.13 us -> 1.04 us
where the time goes in v3:
time: 148 us; the launch traced here: 147 us
  blocking collectives  63.1 us (43%)
  Pallas kernels  49.1 us (33%)
  starting transfers between devices  14.5 us (10%)
  waiting for transfers between devices  13.5 us (9%)
  other arithmetic  3.7 us (2%)
  local copies, waits for them, and re-layouts  2.44 us (2%)
    all_to_all x3, blocking collectives, exchange(): return lax.all_to_all(array, axes, split_axis=0, concat_axis=0, tiled=True)  63.1 us
    pallas_call x1, Pallas kernels, body(): pl.pallas_call(main_kernel, in_specs=[SMEM] * 3 + [VMEM] * 8, out_specs=[...  31.1 us
    pallas_call x1, Pallas kernels, body(): pix, weights, bounds, masks = ordering(pointing, trig)  11.7 us
    all_to_all x1, starting transfers between devices, exchange(): return lax.all_to_all(array, axes, split_axis=0, concat_axis=0, tiled=True)  9.72 us
    all_to_all x1, waiting for transfers between devices, exchange(): return lax.all_to_all(array, axes, split_axis=0, concat_axis=0, tiled=True)  6.99 us
    ppermute x3, starting transfers between devices, body(): lax.ppermute(own, ROW, [(j, (j + s) % n_row) for j in range(n_row)])  3.67 us
    ppermute x3, waiting for transfers between devices, body(): lax.ppermute(own, ROW, [(j, (j + s) % n_row) for j in range(n_row)])  3.53 us
    ppermute x1, waiting for transfers between devices, body(): lax.ppermute(send, CORE, [(0, 1), (1, 0)])  2.99 us
  transfers between devices with their start and end apart: 6, of which 4 were waited for; matrix products, arithmetic and copies ran while one was open for 2% of the time, Pallas kernels for 8%

profile of v3, /device:TPU:1, one launch (start us, length us, event | category | flops | bytes accessed | tf_op | source)
XLA Modules:
  0.0 147.0 jit_solution(11137456810518458054)
XLA Ops:
  0.6 2.2 %shard_map.138 = s32[1536,128]{1,0:T(8,128)} custom-call(s32[32,2048]{1,0:T(8,128)} %pixels_ref.1, s32[32,2048]{1,0:T(8,128)} %angle_ref.1, s32[32,2048]{1,0:T(8,128)} %flag_ref.1), custom_call_target="tpu_custom_call" | custom-call | tf_op jit(solution)/shard_map/pallas_call | solution.py:481
  2.9 0.0 copy-start.3
  2.9 9.7 %all-to-all-start = ((s32[32,3,16,128]{3,2,1,0:T(8,128)}), s32[32,3,16,128]{3,2,1,0:T(8,128)S(1)}, u32[]{:S(2)}, u32[]{:S(2)}) async-start(s32[32,3,16,128]{3,2,1,0:T(8,128)} %bitcast.13), calls=%async_computation | async-start | bytes 1572864 | tf_op jit(solution)/shard_map/all_to_all | solution.py:29
  12.6 0.0 copy-done.3
  12.6 2.5 %collective-permute-start.2 = (f32[36,128]{1,0:T(8,128)S(1)}, f32[36,128]{1,0:T(8,128)S(1)}, u32[]{:S(2)}, u32[]{:S(2)}) collective-permute-start(f32[36,128]{1,0:T(8,128)S(1)} %reshape.56), channel_id=1, source_target_pairs={{0,96},{32,0},{64,32},{96,64},{1,97},{33,1},{65,33},{97,65},{2,98}... | collective-permute-start | bytes 55304 | tf_op jit(solution)/shard_map/ppermute | solution.py:488
  15.2 0.5 collective-permute-start.1
  15.7 0.6 collective-permute-start
  16.3 0.0 collective-permute-done.2
  16.3 3.3 %collective-permute-done.1 = f32[36,128]{1,0:T(8,128)S(1)} collective-permute-done((f32[36,128]{1,0:T(8,128)S(1)}, f32[36,128]{1,0:T(8,128)S(1)}, u32[]{:S(2)}, u32[]{:S(2)}) %collective-permute-start.1) | collective-permute-done | bytes 18464 | tf_op jit(solution)/shard_map/ppermute | solution.py:488
  19.6 0.2 collective-permute-done
  19.8 7.0 %all-to-all-done.pointing_ref = s32[32,3,16,128]{3,2,1,0:T(8,128)S(1)} async-done(((s32[32,3,16,128]{3,2,1,0:T(8,128)}), s32[32,3,16,128]{3,2,1,0:T(8,128)S(1)}, u32[]{:S(2)}, u32[]{:S(2)}) %all-to-all-start) | async-done | bytes 786464 | tf_op jit(solution)/shard_map/all_to_all | solution.py:29
  26.8 0.0 copy-start.1
  26.8 0.1 broadcast_in_dim.5
  26.9 0.0 copy-start.4
  26.9 0.0 copy-start.5
  26.9 0.0 copy-start.6
  27.0 21.9 %all_to_all.20.mine_ref = f32[16,144,128]{2,1,0:T(8,128)S(1)} all-to-all(f32[16,144,128]{2,1,0:T(8,128)S(1)} %broadcast_in_dim.5), channel_id=1, replica_groups=mesh['det'=4,'tm_0'=4,'tm_1'=4,'tm_2'=2] {'tm_0','tm_1'}, dimensions={0} | all-to-all | bytes 2359296 | tf_op jit(solution)/shard_map/all_to_all | solution.py:29
  48.8 0.0 copy-done.1
  48.8 0.0 copy-start
  48.8 1.0 collective-permute-start.3
  49.8 0.0 copy-done.4
  49.8 0.5 fusion
  50.3 0.0 copy-done.5
  50.3 1.1 select_reduce_fusion
  51.5 0.8 copy.15
  52.2 0.6 pad_add_fusion.here_ref
  52.8 0.0 copy-done.6
  52.9 0.6 pad_maximum_fusion.1.trig_ref
  53.4 11.7 %shard_map.139 = (s32[128,512]{1,0:T(8,128)}, f32[3,128,512]{2,1,0:T(8,128)}, s32[4,128]{1,0:T(4,128)}, s32[272,8,128]{2,1,0:T(8,128)}) custom-call(s32[32,3,16,128]{3,2,1,0:T(8,128)} %copy-done.1, f32[2,128]{1,0:T(2,128)} %pad_maximum_fusion.1.trig_ref), custom_call_target="tpu_custom_call" | custom-call | tf_op jit(solution)/shard_map/pallas_call | solution.py:511
  65.2 0.0 collective-permute-done.3.peer_ref
  65.2 0.0 copy-start.2
  65.2 0.0 copy-done
  65.2 1.0 copy-done.2
  66.2 31.1 %shard_map.140 = (f32[2304,128]{1,0:T(8,128)}, f32[2304,128]{1,0:T(8,128)}) custom-call(s32[4,128]{1,0:T(4,128)} %get-tuple-element.31.bound_ref, f32[1]{0:T(128)} %bitcast.3.tail_ref, s32[2]{0:T(128)} %pad_add_fusion.here_ref, s32[128,512]{1,0:T(8,128)} %get-tuple-element.32.pix_ref, f32[3,128,512]{2,1,0:T(8,128)} %get-tuple-element.33.weight_ref, ...), custom_call_target="tpu_custom_call" | custom-call | tf_op jit(solution)/shard_map/pallas_call | solution.py:517
  97.2 0.1 collective-permute-start.4
  97.3 3.0 %collective-permute-done.4 = f32[2304,128]{1,0:T(8,128)S(1)} collective-permute-done((f32[2304,128]{1,0:T(8,128)}, f32[2304,128]{1,0:T(8,128)S(1)}, u32[]{:S(2)}, u32[]{:S(2)}) %collective-permute-start.4) | collective-permute-done | bytes 1179680 | tf_op jit(solution)/shard_map/ppermute | solution.py:525
  100.3 1.4 add.5
  101.7 24.9 %all_to_all.21.shares_ref = f32[64,9,4,128]{3,2,1,0:T(4,128)} all-to-all(f32[64,9,4,128]{3,2,1,0:T(4,128)S(1)} %bitcast.12), channel_id=1, replica_groups=mesh['det'=4,'tm_0'=4,'tm_1'=4,'tm_2'=2] {'det','tm_0','tm_1'}, dimensions={0} | all-to-all | bytes 2359296 | tf_op jit(solution)/shard_map/all_to_all | solution.py:29
  126.6 2.3 %shard_map.141 = (f32[3,1536]{1,0:T(4,128)}, f32[128,1,128]{2,1,0:T(1,128)}) custom-call(f32[64,9,4,128]{3,2,1,0:T(4,128)} %all_to_all.21.shares_ref, f32[3,1536]{1,0:T(4,128)} %resid_ref.3, f32[3,1536]{1,0:T(4,128)} %direction_ref.3, f32[3,1536]{1,0:T(4,128)} %precond_ref.3), custom_call_target="tpu_custom_call" | custom-call | tf_op jit(solution)/shard_map/pallas_call | solution.py:527
  128.9 16.3 %all_to_all.22.sums_ref = f32[128,1,128]{2,1,0:T(1,128)} all-to-all(f32[128,1,128]{2,1,0:T(1,128)} %get-tuple-element.38), channel_id=1, replica_groups=mesh['det'=4,'tm_0'=4,'tm_1'=4,'tm_2'=2] {'det','tm_0','tm_1','tm_2'}, dimensions={0} | all-to-all | bytes 131072 | tf_op jit(solution)/shard_map/all_to_all | solution.py:29
  145.2 1.7 %shard_map.142 = (f32[3,1536]{1,0:T(4,128)}, f32[3,1536]{1,0:T(4,128)}, f32[3,1536]{1,0:T(4,128)}, f32[1,1]{1,0:T(1,128)}) custom-call(f32[128,1,128]{2,1,0:T(1,128)} %all_to_all.22.sums_ref, f32[3,1536]{1,0:T(4,128)} %get-tuple-element.39.image_ref, f32[3,1536]{1,0:T(4,128)} %sol_ref.1, f32[3,1536]{1,0:T(4,128)} %resid_ref.3, f32[3,1536]{1,0:T(4,128)} %direction_ref.3, ...), custom_call_target="tpu_custom_call" | custom-call | tf_op jit(solution)/shard_map/pallas_call | solution.py:530
  (4 shorter events, 0.1 us)
Async XLA Ops:
  2.9 9.7 %copy-start.3 = (f32[3,1536]{1,0:T(4,128)S(1)}, f32[3,1536]{1,0:T(4,128)}, u32[]{:S(2)}) copy-start(f32[3,1536]{1,0:T(4,128)} %direction_ref.3) | copy-start | bytes 55300
  2.9 24.0 %all-to-all-start = ((s32[32,3,16,128]{3,2,1,0:T(8,128)}), s32[32,3,16,128]{3,2,1,0:T(8,128)S(1)}, u32[]{:S(2)}, u32[]{:S(2)}) async-start(s32[32,3,16,128]{3,2,1,0:T(8,128)} %bitcast.13), calls=%async_computation | async-start | bytes 1572864 | tf_op jit(solution)/shard_map/all_to_all | solution.py:29
  12.6 3.7 %collective-permute-start.2 = (f32[36,128]{1,0:T(8,128)S(1)}, f32[36,128]{1,0:T(8,128)S(1)}, u32[]{:S(2)}, u32[]{:S(2)}) collective-permute-start(f32[36,128]{1,0:T(8,128)S(1)} %reshape.56), channel_id=1, source_target_pairs={{0,96},{32,0},{64,32},{96,64},{1,97},{33,1},{65,33},{97,65},{2,98}... | collective-permute-start | bytes 55304 | tf_op jit(solution)/shard_map/ppermute | solution.py:488
  15.2 4.4 %collective-permute-start.1 = (f32[36,128]{1,0:T(8,128)S(1)}, f32[36,128]{1,0:T(8,128)S(1)}, u32[]{:S(2)}, u32[]{:S(2)}) collective-permute-start(f32[36,128]{1,0:T(8,128)S(1)} %reshape.56), channel_id=1, source_target_pairs={{0,64},{32,96},{64,0},{96,32},{1,65},{33,97},{65,1},{97,33},{2,66}... | collective-permute-start | bytes 55304 | tf_op jit(solution)/shard_map/ppermute | solution.py:488
  15.7 4.1 %collective-permute-start = (f32[36,128]{1,0:T(8,128)S(1)}, f32[36,128]{1,0:T(8,128)S(1)}, u32[]{:S(2)}, u32[]{:S(2)}) collective-permute-start(f32[36,128]{1,0:T(8,128)S(1)} %reshape.56), channel_id=1, source_target_pairs={{0,32},{32,64},{64,96},{96,0},{1,33},{33,65},{65,97},{97,1},{2,34}... | collective-permute-start | bytes 55304 | tf_op jit(solution)/shard_map/ppermute | solution.py:488
  26.8 22.0 %copy-start.1 = (s32[32,3,16,128]{3,2,1,0:T(8,128)}, s32[32,3,16,128]{3,2,1,0:T(8,128)S(1)}, u32[]{:S(2)}) copy-start(s32[32,3,16,128]{3,2,1,0:T(8,128)S(1)} %all-to-all-done.pointing_ref) | copy-start | bytes 2359300
  26.9 22.9 %copy-start.4 = (f32[1,32769]{1,0:T(1,128)S(1)}, f32[1,32769]{1,0:T(1,128)}, u32[]{:S(2)}) copy-start(f32[1,32769]{1,0:T(1,128)} %param.21) | copy-start | bytes 393232
  26.9 23.4 %copy-start.5 = (pred[1,32768]{1,0:T(4,128)(4,1)S(1)}, pred[1,32768]{1,0:T(4,128)(4,1)}, u32[]{:S(2)}) copy-start(pred[1,32768]{1,0:T(4,128)(4,1)} %constant.51.clone.1) | copy-start | bytes 98308
  26.9 25.9 %copy-start.6 = (f32[128]{0:T(128)S(1)}, f32[128]{0:T(128)}, u32[]{:S(2)}) copy-start(f32[128]{0:T(128)} %param.19) | copy-start | bytes 1540
  48.8 16.4 %copy-start = (f32[16,144,128]{2,1,0:T(8,128)}, f32[16,144,128]{2,1,0:T(8,128)S(1)}, u32[]{:S(2)}) copy-start(f32[16,144,128]{2,1,0:T(8,128)S(1)} %all_to_all.20.mine_ref) | copy-start | bytes 3538948
  48.8 16.4 %collective-permute-start.3 = (f32[16,144,128]{2,1,0:T(8,128)S(1)}, f32[16,144,128]{2,1,0:T(8,128)S(1)}, u32[]{:S(2)}, u32[]{:S(2)}) collective-permute-start(f32[16,144,128]{2,1,0:T(8,128)S(1)} %all_to_all.20.mine_ref), channel_id=1, source_target_pairs={{0,1},{1,0},{2,3},{3,2},{4,5},{5,4},{6,7},{7,6},{8,9},{9,8},{10,11... | collective-permute-start | bytes 3538952 | tf_op jit(solution)/shard_map/ppermute | solution.py:494
  65.2 1.0 copy-start.2
  97.2 3.1 %collective-permute-start.4 = (f32[2304,128]{1,0:T(8,128)}, f32[2304,128]{1,0:T(8,128)S(1)}, u32[]{:S(2)}, u32[]{:S(2)}) collective-permute-start(f32[2304,128]{1,0:T(8,128)} %get-tuple-element.37), channel_id=1, source_target_pairs={{0,1},{1,0},{2,3},{3,2},{4,5},{5,4},{6,7},{7,6},{8,9},{9,8},{10,11... | collective-permute-start | bytes 3538952 | tf_op jit(solution)/shard_map/ppermute | solution.py:525

commit v4 on v3

--- a/solution.py
+++ b/solution.py
@@ -23,6 +23,7 @@
 ROWS = 32
 VMEM = pl.BlockSpec(memory_space=pltpu.VMEM)
 SMEM = pl.BlockSpec(memory_space=pltpu.SMEM)
+LATE = pl.BlockSpec(memory_space=pl.ANY)
 
 
 def exchange(array, axes):
@@ -325,9 +326,13 @@
 
 
 def main_kernel(
-    bound_ref, tail_ref, here_ref, pix_ref, weight_ref, mask_ref, mine_ref, peer_ref, form_ref, twist_ref, filt_ref, keep_ref, send_ref, *scratch
+    bound_ref, tail_ref, here_ref, pix_ref, weight_ref, mask_src, mine_ref, peer_ref, form_src, twist_src, filt_src, keep_ref, send_ref, *scratch
 ):
-    tab_ref, series_ref, wide_ref = scratch
+    tab_ref, series_ref, wide_ref, mask_ref, form_ref, twist_ref, filt_ref, arrived = scratch
+    late = ((mask_src, mask_ref), (form_src, form_ref), (twist_src, twist_ref), (filt_src, filt_ref))
+    late = [pltpu.make_async_copy(src, dst, arrived.at[i]) for i, (src, dst) in enumerate(late)]
+    for copy in late:
+        copy.start()
     n_row = 4
     plane = mine_ref.shape[0]
     per_share = mine_ref.shape[1] // n_row
@@ -350,6 +355,8 @@
     tab_ref[:, map_rows:, :] = jnp.zeros((3, tab_ref.shape[1] - map_rows, LANES), jnp.float32)
 
     gather_all(bound_ref, pix_ref, weight_ref, tab_ref, wide_ref)
+    for copy in late:
+        copy.wait()
     for part in range(4):
         series_ref[part * LANES : (part + 1) * LANES, :] = wide_ref[:, part * LANES : (part + 1) * LANES].T
     network(replay_stage, series_ref, mask_ref, backwards=True)
@@ -516,10 +523,16 @@
     halved = jax.ShapeDtypeStruct((n_dev // 2 * 3 * share_rows, LANES), f32)
     keep, send = pl.pallas_call(
         main_kernel,
-        in_specs=[SMEM] * 3 + [VMEM] * 8,
+        in_specs=[SMEM] * 3 + [VMEM] * 2 + [LATE] + [VMEM] * 2 + [LATE] * 3,
         out_specs=[VMEM] * 2,
         out_shape=[halved] * 2,
-        scratch_shapes=[pltpu.VMEM((3, map_rows + 8, LANES), f32), pltpu.VMEM((total // LANES, LANES), f32), pltpu.VMEM(wide, f32)],
+        scratch_shapes=[
+            pltpu.VMEM((3, map_rows + 8, LANES), f32),
+            pltpu.VMEM((total // LANES, LANES), f32),
+            pltpu.VMEM(wide, f32),
+            *[pltpu.VMEM(a.shape, a.dtype) for a in (masks, forms, twists, doubled)],
+            pltpu.SemaphoreType.DMA((4,)),
+        ],
     )(bounds, inv_noise[0, total // 2 :], here, pix, weights, masks, mine, peer, forms, twists, doubled)
 
     shares = (keep + lax.ppermute(send, CORE, [(0, 1), (1, 0)])).reshape(n_dev // 2, 3 * share_rows // 4, 4, LANES)

time: 148 us -> 147 us (level)
  no operation moved by 1% of the time
where the time goes in v4:
time: 147 us; the launch traced here: 146 us
  blocking collectives  63.1 us (43%)
  Pallas kernels  48.5 us (33%)
  starting transfers between devices  14.5 us (10%)
  waiting for transfers between devices  13.5 us (9%)
  other arithmetic  3.7 us (3%)
  local copies, waits for them, and re-layouts  2.44 us (2%)
    all_to_all x3, blocking collectives, exchange(): return lax.all_to_all(array, axes, split_axis=0, concat_axis=0, tiled=True)  63.1 us
    pallas_call x1, Pallas kernels, body(): pl.pallas_call(main_kernel, in_specs=[SMEM] * 3 + [VMEM] * 2 + [LATE] + [...  30.5 us
    pallas_call x1, Pallas kernels, body(): pix, weights, bounds, masks = ordering(pointing, trig)  11.7 us
    all_to_all x1, starting transfers between devices, exchange(): return lax.all_to_all(array, axes, split_axis=0, concat_axis=0, tiled=True)  9.72 us
    all_to_all x1, waiting for transfers between devices, exchange(): return lax.all_to_all(array, axes, split_axis=0, concat_axis=0, tiled=True)  6.99 us
    ppermute x3, starting transfers between devices, body(): lax.ppermute(own, ROW, [(j, (j + s) % n_row) for j in range(n_row)])  3.67 us
    ppermute x3, waiting for transfers between devices, body(): lax.ppermute(own, ROW, [(j, (j + s) % n_row) for j in range(n_row)])  3.53 us
    ppermute x1, waiting for transfers between devices, body(): lax.ppermute(send, CORE, [(0, 1), (1, 0)])  2.99 us
  transfers between devices with their start and end apart: 6, of which 4 were waited for; matrix products, arithmetic and copies ran while one was open for 2% of the time, Pallas kernels for 8%

profile of v4, /device:TPU:1, one launch (start us, length us, event | category | flops | bytes accessed | tf_op | source)
XLA Modules:
  0.0 146.5 jit_solution(9747888899337052949)
XLA Ops:
  0.6 2.2 %shard_map.138 = s32[1536,128]{1,0:T(8,128)} custom-call(s32[32,2048]{1,0:T(8,128)} %pixels_ref.1, s32[32,2048]{1,0:T(8,128)} %angle_ref.1, s32[32,2048]{1,0:T(8,128)} %flag_ref.1), custom_call_target="tpu_custom_call" | custom-call | tf_op jit(solution)/shard_map/pallas_call | solution.py:488
  2.9 0.0 copy-start.3
  2.9 9.7 %all-to-all-start = ((s32[32,3,16,128]{3,2,1,0:T(8,128)}), s32[32,3,16,128]{3,2,1,0:T(8,128)S(1)}, u32[]{:S(2)}, u32[]{:S(2)}) async-start(s32[32,3,16,128]{3,2,1,0:T(8,128)} %bitcast.13), calls=%async_computation | async-start | bytes 1572864 | tf_op jit(solution)/shard_map/all_to_all | solution.py:30
  12.6 0.0 copy-done.3
  12.6 2.5 %collective-permute-start.2 = (f32[36,128]{1,0:T(8,128)S(1)}, f32[36,128]{1,0:T(8,128)S(1)}, u32[]{:S(2)}, u32[]{:S(2)}) collective-permute-start(f32[36,128]{1,0:T(8,128)S(1)} %reshape.56), channel_id=1, source_target_pairs={{0,96},{32,0},{64,32},{96,64},{1,97},{33,1},{65,33},{97,65},{2,98}... | collective-permute-start | bytes 55304 | tf_op jit(solution)/shard_map/ppermute | solution.py:495
  15.2 0.5 collective-permute-start.1
  15.7 0.6 collective-permute-start
  16.3 0.0 collective-permute-done.2
  16.3 3.3 %collective-permute-done.1 = f32[36,128]{1,0:T(8,128)S(1)} collective-permute-done((f32[36,128]{1,0:T(8,128)S(1)}, f32[36,128]{1,0:T(8,128)S(1)}, u32[]{:S(2)}, u32[]{:S(2)}) %collective-permute-start.1) | collective-permute-done | bytes 18464 | tf_op jit(solution)/shard_map/ppermute | solution.py:495
  19.6 0.2 collective-permute-done
  19.8 7.0 %all-to-all-done.pointing_ref = s32[32,3,16,128]{3,2,1,0:T(8,128)S(1)} async-done(((s32[32,3,16,128]{3,2,1,0:T(8,128)}), s32[32,3,16,128]{3,2,1,0:T(8,128)S(1)}, u32[]{:S(2)}, u32[]{:S(2)}) %all-to-all-start) | async-done | bytes 786464 | tf_op jit(solution)/shard_map/all_to_all | solution.py:30
  26.8 0.0 copy-start.1
  26.8 0.1 broadcast_in_dim.5
  26.9 0.0 copy-start.4
  26.9 0.0 copy-start.5
  26.9 0.0 copy-start.6
  27.0 21.9 %all_to_all.20.mine_ref = f32[16,144,128]{2,1,0:T(8,128)S(1)} all-to-all(f32[16,144,128]{2,1,0:T(8,128)S(1)} %broadcast_in_dim.5), channel_id=1, replica_groups=mesh['det'=4,'tm_0'=4,'tm_1'=4,'tm_2'=2] {'tm_0','tm_1'}, dimensions={0} | all-to-all | bytes 2359296 | tf_op jit(solution)/shard_map/all_to_all | solution.py:30
  48.8 0.0 copy-done.1
  48.8 0.0 copy-start
  48.8 1.0 collective-permute-start.3
  49.8 0.0 copy-done.4
  49.8 0.5 fusion
  50.3 0.0 copy-done.5
  50.3 1.1 select_reduce_fusion
  51.5 0.8 copy.15
  52.2 0.6 pad_add_fusion.here_ref
  52.8 0.0 copy-done.6
  52.9 0.6 pad_maximum_fusion.1.trig_ref
  53.4 11.7 %shard_map.139 = (s32[128,512]{1,0:T(8,128)}, f32[3,128,512]{2,1,0:T(8,128)}, s32[4,128]{1,0:T(4,128)}, s32[272,8,128]{2,1,0:T(8,128)}) custom-call(s32[32,3,16,128]{3,2,1,0:T(8,128)} %copy-done.1, f32[2,128]{1,0:T(2,128)} %pad_maximum_fusion.1.trig_ref), custom_call_target="tpu_custom_call" | custom-call | tf_op jit(solution)/shard_map/pallas_call | solution.py:518
  65.2 0.0 collective-permute-done.3.peer_ref
  65.2 0.0 copy-start.2
  65.2 0.0 copy-done
  65.2 1.0 copy-done.2
  66.2 30.5 %shard_map.140 = (f32[2304,128]{1,0:T(8,128)}, f32[2304,128]{1,0:T(8,128)}) custom-call(s32[4,128]{1,0:T(4,128)} %get-tuple-element.31.bound_ref, f32[1]{0:T(128)} %bitcast.3.tail_ref, s32[2]{0:T(128)} %pad_add_fusion.here_ref, s32[128,512]{1,0:T(8,128)} %get-tuple-element.32.pix_ref, f32[3,128,512]{2,1,0:T(8,128)} %get-tuple-element.33.weight_ref, ...), custom_call_target="tpu_custom_call" | custom-call | tf_op jit(solution)/shard_map/pallas_call | solution.py:524
  96.7 0.2 collective-permute-start.4
  96.8 3.0 %collective-permute-done.4 = f32[2304,128]{1,0:T(8,128)S(1)} collective-permute-done((f32[2304,128]{1,0:T(8,128)}, f32[2304,128]{1,0:T(8,128)S(1)}, u32[]{:S(2)}, u32[]{:S(2)}) %collective-permute-start.4) | collective-permute-done | bytes 1179680 | tf_op jit(solution)/shard_map/ppermute | solution.py:538
  99.8 1.4 add.5
  101.2 24.9 %all_to_all.21.shares_ref = f32[64,9,4,128]{3,2,1,0:T(4,128)} all-to-all(f32[64,9,4,128]{3,2,1,0:T(4,128)S(1)} %bitcast.12), channel_id=1, replica_groups=mesh['det'=4,'tm_0'=4,'tm_1'=4,'tm_2'=2] {'det','tm_0','tm_1'}, dimensions={0} | all-to-all | bytes 2359296 | tf_op jit(solution)/shard_map/all_to_all | solution.py:30
  126.1 2.3 %shard_map.141 = (f32[3,1536]{1,0:T(4,128)}, f32[128,1,128]{2,1,0:T(1,128)}) custom-call(f32[64,9,4,128]{3,2,1,0:T(4,128)} %all_to_all.21.shares_ref, f32[3,1536]{1,0:T(4,128)} %resid_ref.3, f32[3,1536]{1,0:T(4,128)} %direction_ref.3, f32[3,1536]{1,0:T(4,128)} %precond_ref.3), custom_call_target="tpu_custom_call" | custom-call | tf_op jit(solution)/shard_map/pallas_call | solution.py:540
  128.4 16.3 %all_to_all.22.sums_ref = f32[128,1,128]{2,1,0:T(1,128)} all-to-all(f32[128,1,128]{2,1,0:T(1,128)} %get-tuple-element.38), channel_id=1, replica_groups=mesh['det'=4,'tm_0'=4,'tm_1'=4,'tm_2'=2] {'det','tm_0','tm_1','tm_2'}, dimensions={0} | all-to-all | bytes 131072 | tf_op jit(solution)/shard_map/all_to_all | solution.py:30
  144.7 1.7 %shard_map.142 = (f32[3,1536]{1,0:T(4,128)}, f32[3,1536]{1,0:T(4,128)}, f32[3,1536]{1,0:T(4,128)}, f32[1,1]{1,0:T(1,128)}) custom-call(f32[128,1,128]{2,1,0:T(1,128)} %all_to_all.22.sums_ref, f32[3,1536]{1,0:T(4,128)} %get-tuple-element.39.image_ref, f32[3,1536]{1,0:T(4,128)} %sol_ref.1, f32[3,1536]{1,0:T(4,128)} %resid_ref.3, f32[3,1536]{1,0:T(4,128)} %direction_ref.3, ...), custom_call_target="tpu_custom_call" | custom-call | tf_op jit(solution)/shard_map/pallas_call | solution.py:543
  (4 shorter events, 0.1 us)
Async XLA Ops:
  2.9 9.7 %copy-start.3 = (f32[3,1536]{1,0:T(4,128)S(1)}, f32[3,1536]{1,0:T(4,128)}, u32[]{:S(2)}) copy-start(f32[3,1536]{1,0:T(4,128)} %direction_ref.3) | copy-start | bytes 55300
  2.9 24.0 %all-to-all-start = ((s32[32,3,16,128]{3,2,1,0:T(8,128)}), s32[32,3,16,128]{3,2,1,0:T(8,128)S(1)}, u32[]{:S(2)}, u32[]{:S(2)}) async-start(s32[32,3,16,128]{3,2,1,0:T(8,128)} %bitcast.13), calls=%async_computation | async-start | bytes 1572864 | tf_op jit(solution)/shard_map/all_to_all | solution.py:30
  12.6 3.7 %collective-permute-start.2 = (f32[36,128]{1,0:T(8,128)S(1)}, f32[36,128]{1,0:T(8,128)S(1)}, u32[]{:S(2)}, u32[]{:S(2)}) collective-permute-start(f32[36,128]{1,0:T(8,128)S(1)} %reshape.56), channel_id=1, source_target_pairs={{0,96},{32,0},{64,32},{96,64},{1,97},{33,1},{65,33},{97,65},{2,98}... | collective-permute-start | bytes 55304 | tf_op jit(solution)/shard_map/ppermute | solution.py:495
  15.2 4.4 %collective-permute-start.1 = (f32[36,128]{1,0:T(8,128)S(1)}, f32[36,128]{1,0:T(8,128)S(1)}, u32[]{:S(2)}, u32[]{:S(2)}) collective-permute-start(f32[36,128]{1,0:T(8,128)S(1)} %reshape.56), channel_id=1, source_target_pairs={{0,64},{32,96},{64,0},{96,32},{1,65},{33,97},{65,1},{97,33},{2,66}... | collective-permute-start | bytes 55304 | tf_op jit(solution)/shard_map/ppermute | solution.py:495
  15.7 4.1 %collective-permute-start = (f32[36,128]{1,0:T(8,128)S(1)}, f32[36,128]{1,0:T(8,128)S(1)}, u32[]{:S(2)}, u32[]{:S(2)}) collective-permute-start(f32[36,128]{1,0:T(8,128)S(1)} %reshape.56), channel_id=1, source_target_pairs={{0,32},{32,64},{64,96},{96,0},{1,33},{33,65},{65,97},{97,1},{2,34}... | collective-permute-start | bytes 55304 | tf_op jit(solution)/shard_map/ppermute | solution.py:495
  26.8 22.0 %copy-start.1 = (s32[32,3,16,128]{3,2,1,0:T(8,128)}, s32[32,3,16,128]{3,2,1,0:T(8,128)S(1)}, u32[]{:S(2)}) copy-start(s32[32,3,16,128]{3,2,1,0:T(8,128)S(1)} %all-to-all-done.pointing_ref) | copy-start | bytes 2359300
  26.9 22.9 %copy-start.4 = (f32[1,32769]{1,0:T(1,128)S(1)}, f32[1,32769]{1,0:T(1,128)}, u32[]{:S(2)}) copy-start(f32[1,32769]{1,0:T(1,128)} %param.21) | copy-start | bytes 393232
  26.9 23.4 %copy-start.5 = (pred[1,32768]{1,0:T(4,128)(4,1)S(1)}, pred[1,32768]{1,0:T(4,128)(4,1)}, u32[]{:S(2)}) copy-start(pred[1,32768]{1,0:T(4,128)(4,1)} %constant.51.clone.1) | copy-start | bytes 98308
  26.9 25.9 %copy-start.6 = (f32[128]{0:T(128)S(1)}, f32[128]{0:T(128)}, u32[]{:S(2)}) copy-start(f32[128]{0:T(128)} %param.19) | copy-start | bytes 1540
  48.8 16.4 %copy-start = (f32[16,144,128]{2,1,0:T(8,128)}, f32[16,144,128]{2,1,0:T(8,128)S(1)}, u32[]{:S(2)}) copy-start(f32[16,144,128]{2,1,0:T(8,128)S(1)} %all_to_all.20.mine_ref) | copy-start | bytes 3538948
  48.8 16.4 %collective-permute-start.3 = (f32[16,144,128]{2,1,0:T(8,128)S(1)}, f32[16,144,128]{2,1,0:T(8,128)S(1)}, u32[]{:S(2)}, u32[]{:S(2)}) collective-permute-start(f32[16,144,128]{2,1,0:T(8,128)S(1)} %all_to_all.20.mine_ref), channel_id=1, source_target_pairs={{0,1},{1,0},{2,3},{3,2},{4,5},{5,4},{6,7},{7,6},{8,9},{9,8},{10,11... | collective-permute-start | bytes 3538952 | tf_op jit(solution)/shard_map/ppermute | solution.py:501
  65.2 1.0 copy-start.2
  96.7 3.1 %collective-permute-start.4 = (f32[2304,128]{1,0:T(8,128)}, f32[2304,128]{1,0:T(8,128)S(1)}, u32[]{:S(2)}, u32[]{:S(2)}) collective-permute-start(f32[2304,128]{1,0:T(8,128)} %get-tuple-element.37), channel_id=1, source_target_pairs={{0,1},{1,0},{2,3},{3,2},{4,5},{5,4},{6,7},{7,6},{8,9},{9,8},{10,11... | collective-permute-start | bytes 3538952 | tf_op jit(solution)/shard_map/ppermute | solution.py:538
